TPU v7x, 32 devices: a whole 2x2x4 slice. The times are simulated.
32 devices in a mesh: fsdp: 4 (over y, x), tensor: 8 (over z, core).
Axes of the slice: x: 2, y: 2, z: 4, core: 2. Of those that a mesh axis runs over, the one named last changes fastest.
Arguments:
- modality: int32 [4096], P('fsdp'), may hold values from 0 to 2, as said below
- out_grad: bfloat16 [4096, 4096], P('fsdp', 'tensor'), may hold values from -6 to 6
- gate_pre: bfloat16 [4096, 11008], P('fsdp', 'tensor'), may hold values from -6 to 6
- up_pre: bfloat16 [4096, 11008], P('fsdp', 'tensor'), may hold values from -6 to 6
- down_weight: bfloat16 [3, 11008, 4096], P(None, 'tensor', 'fsdp'), may hold values from -0.0546875 to 0.0546875
Outputs:
- down_grad: float32 [3, 11008, 4096], P(None, 'tensor', 'fsdp')
- gate_grad: bfloat16 [4096, 11008], P('fsdp', 'tensor')
- up_grad: bfloat16 [4096, 11008], P('fsdp', 'tensor')
Inputs may be any that keep to these rules, and one draw needn't show every extreme that they name: `modality`: the 1024 tokens of every index of fsdp hold each of the three modalities at least once.
All inputs are finite; a program needn't handle non-finite values.
Results may differ from a plain program's by a relative error of at most 0.012.
Values may be sent and summed in bfloat16 or wider, within the bound.
A program may use at most 256 MiB of HBM per device.

v0:
```python
import functools

import jax
import jax.numpy as jnp
from jax import lax
from jax.experimental import pallas as pl
from jax.experimental.pallas import tpu as pltpu
from jax.sharding import PartitionSpec as P


def kind_table(kind_ids):
    labels = jnp.arange(3, dtype=jnp.int32)
    return (kind_ids[:, None] == labels[None, :]).astype(jnp.float32)


def swap(values, axis, size, step):
    return lax.ppermute(values, axis, [(i, i ^ step) for i in range(size)])


def activations(gate_pre, up_pre):
    gate_val = gate_pre.astype(jnp.float32)
    up_val = up_pre.astype(jnp.float32)
    sigmoid_g = jax.nn.sigmoid(gate_val)
    return gate_val, up_val, sigmoid_g, gate_val * sigmoid_g


def hidden_of(gate_pre, up_pre):
    _, up_val, _, active = activations(gate_pre, up_pre)
    return (active * up_val).astype(jnp.bfloat16)


def grads_of(folded, gate_pre, up_pre):
    gate_val, up_val, sigmoid_g, active = activations(gate_pre, up_pre)
    up_grad = (folded * active).astype(jnp.bfloat16)
    slope = sigmoid_g * (1.0 + gate_val * (1.0 - sigmoid_g))
    gate_grad = (folded * up_val * slope).astype(jnp.bfloat16)
    return gate_grad, up_grad


def masked_back(scaled, onehot, down_weight):
    marks = onehot.T.astype(jnp.bfloat16)
    masked = scaled[None, :, :] * marks[:, :, None]
    return lax.dot_general(
        masked, down_weight, (((0, 2), (0, 2)), ((), ())), preferred_element_type=jnp.float32
    )


def weight_grad(hid_all, scaled_all, onehot_all):
    marks_all = onehot_all.T.astype(jnp.bfloat16)
    masked_all = scaled_all[None, :, :] * marks_all[:, :, None]
    stacked = jnp.broadcast_to(hid_all[None, :, :], (3,) + hid_all.shape)
    return lax.dot_general(
        stacked, masked_all, (((1,), (1,)), ((0,), (0,))), preferred_element_type=jnp.float32
    )


HBM = pltpu.MemorySpace.HBM


def weight_body(kinds, owners, tile, *refs):
    pieces = refs[: sum(len(owner) for owner in owners)]
    scaled = refs[len(pieces) : len(pieces) + len(owners)]
    marks_ref = refs[len(pieces) + len(owners)]
    out_ref, hid_buf, scaled_buf, total, hid_sem, scaled_sem, out_sem = refs[-7:]
    chunks = len(owners)
    tiles = total.shape[1] // tile

    def fetch(at, slot, act):
        for c, owner in enumerate(owners):

            @pl.when(at == c)
            def _():
                act(pltpu.make_async_copy(scaled[c], scaled_buf.at[slot], scaled_sem.at[slot]))
                for p, (index, offset, count) in enumerate(owner):
                    here = hid_buf.at[slot, :, pl.ds(offset, count)]
                    act(pltpu.make_async_copy(pieces[index], here, hid_sem.at[slot, p]))

    fetch(0, 0, lambda copy: copy.start())

    def columns(t):
        return pl.ds(pl.multiple_of(t * tile, tile), tile)

    def put(n, t):
        return pltpu.make_async_copy(
            total.at[:, columns(t)], out_ref.at[kinds[0] + n, :, columns(t)], out_sem.at[t]
        )

    def chunk(step, carry):
        n, c = step // chunks, lax.rem(step, chunks)
        slot = lax.rem(step, 2)

        @pl.when(step + 1 < len(kinds) * chunks)
        def _():
            fetch(lax.rem(step + 1, chunks), 1 - slot, lambda copy: copy.start())

        fetch(c, slot, lambda copy: copy.wait())

        def one(t, carry):
            @pl.when((c == 0) & (n > 0))
            def _():
                put(n - 1, t).wait()

            mark = marks_ref[n, c].astype(jnp.bfloat16)
            part = jnp.dot(
                hid_buf[slot] * mark,
                scaled_buf[slot, :, columns(t)],
                preferred_element_type=jnp.float32,
            )
            total[:, columns(t)] = jnp.where(c > 0, total[:, columns(t)], 0.0) + part

            @pl.when(c == chunks - 1)
            def _():
                put(n, t).start()

            return carry

        return lax.fori_loop(0, tiles, one, carry)

    lax.fori_loop(0, len(kinds) * chunks, chunk, 0)
    for t in range(tiles):
        put(len(kinds) - 1, t).wait()


def weight_grad_of(kinds, hidden, scaled, marks, before):
    owners, pieces = [], []
    for owner in hidden:
        listed, offset = [], 0
        for piece in owner:
            listed.append((len(pieces), offset, piece.shape[1]))
            pieces.append(piece)
            offset += piece.shape[1]
        owners.append(tuple(listed))
    rows, cols = scaled[0].shape
    width = pieces[0].shape[0]
    tiles = 2
    hbm = pl.BlockSpec(memory_space=HBM)
    operands = [*pieces, *scaled, marks]
    specs = [hbm] * (len(operands) - 1) + [pl.BlockSpec(memory_space=pltpu.VMEM)]
    aliases = {}
    if before is not None:
        operands.append(before)
        specs.append(hbm)
        aliases = {len(operands) - 1: 0}
    most = max(len(owner) for owner in owners)
    tokens = rows * len(owners)
    return pl.pallas_call(
        functools.partial(weight_body, kinds, tuple(owners), cols // tiles),
        out_shape=jax.ShapeDtypeStruct((3, width, cols), jnp.float32),
        in_specs=specs,
        out_specs=hbm,
        scratch_shapes=[
            pltpu.VMEM((2, width, rows), jnp.bfloat16),
            pltpu.VMEM((2, rows, cols), jnp.bfloat16),
            pltpu.VMEM((width, cols), jnp.float32),
            pltpu.SemaphoreType.DMA((2, most)),
            pltpu.SemaphoreType.DMA((2,)),
            pltpu.SemaphoreType.DMA((tiles,)),
        ],
        input_output_aliases=aliases,
        compiler_params=pltpu.CompilerParams(vmem_limit_bytes=24 * 2**20),
        cost_estimate=pl.CostEstimate(
            flops=2 * len(kinds) * tokens * width * cols,
            bytes_accessed=2 * tokens * (width + cols) + 4 * len(kinds) * width * cols,
            transcendentals=0,
        ),
    )(*operands)


def grads_body(base_ref, direct_ref, got_ref, gate_ref, up_ref, *refs):
    gate_out, up_out = refs[-2:]
    lane = 128

    def one(j, carry):
        at = (slice(None), pl.ds(pl.multiple_of(j * lane, lane), lane))
        folded = base_ref[at] + direct_ref[at].astype(jnp.float32) + got_ref[at].astype(jnp.float32)
        gate_out[at], up_out[at] = grads_of(folded, gate_ref[at], up_ref[at])
        return carry

    lax.fori_loop(0, got_ref.shape[1] // lane, one, 0)


def grads_into(base, direct, first, got, gate_turned, up_turned, column, before):
    width, count = got.shape
    steps = 4 if width % 64 == 0 else 1
    tall = width // steps

    def at(start):
        return pl.BlockSpec((tall, count), lambda i: (i, start // count))

    operands = [base, direct, got, gate_turned, up_turned]
    specs = [at(first), at(first), at(0), at(column), at(column)]
    aliases = {}
    if before is not None:
        operands += before
        specs += [pl.BlockSpec(memory_space=HBM)] * 2
        aliases = {5: 0, 6: 1}
    out = jax.ShapeDtypeStruct(gate_turned.shape, jnp.bfloat16)
    return pl.pallas_call(
        grads_body,
        grid=(steps,),
        out_shape=(out, out),
        in_specs=specs,
        out_specs=(at(column), at(column)),
        input_output_aliases=aliases,
        compiler_params=pltpu.CompilerParams(vmem_limit_bytes=16 * 2**20),
        cost_estimate=pl.CostEstimate(
            flops=20 * width * count,
            bytes_accessed=16 * width * count,
            transcendentals=width * count,
        ),
    )(*operands)


def shards_planes(modality, out_grad, gate_pre, up_pre, down_weight):
    return planes_body(modality, out_grad, gate_pre, up_pre, down_weight)


def planes_body(modality, out_grad, gate_pre, up_pre, down_weight):
    rows, block = out_grad.shape
    groups = lax.axis_size("fsdp")
    lanes = lax.axis_size("tensor")
    planes = lanes // 2
    quarter = rows // planes
    half = rows // 2
    cut = half // 2
    me = lax.axis_index("fsdp")
    lane = lax.axis_index("tensor")
    plane = lane // 2
    core = lane % 2
    gate_turned, up_turned = gate_pre.T, up_pre.T

    def over(values, step):
        return lax.ppermute(values, "fsdp", [(i, i ^ step) for i in range(groups)])

    def along(values, step):
        return lax.ppermute(values, "tensor", [(i, i ^ step) for i in range(lanes)])

    hid_a = hidden_of(gate_turned[:, :half], up_turned[:, :half])
    hid_b = hidden_of(gate_turned[:, half:], up_turned[:, half:])
    hid1b, hid2a = over(hid_b, 1), over(hid_a, 2)
    hid1a, hid2b = over(hid_a, 1), over(hid_b, 2)
    hid3a, hid3b = over(hid2a, 1), over(hid1b, 2)
    hidden = [[hid_a, hid_b], [hid1a, hid1b], [hid2a, hid2b], [hid3a, hid3b]]

    own = out_grad.reshape(planes, quarter, block)
    legs = []
    for d in range(planes):
        part = lax.dynamic_index_in_dim(own, plane ^ d, 0, keepdims=False)
        legs.append(along(part, 2 * d) if d else part)

    kinds = [modality] + [over(modality, k) for k in range(1, groups)]

    stacked = jnp.stack(legs)
    crossed = {}
    for k in (3, 1, 2, 0):
        part = lax.dynamic_index_in_dim(stacked, plane ^ me ^ k, 0, keepdims=False)
        crossed[k] = over(part, k) if k else part

    onehots = [kind_table(kind_ids) for kind_ids in kinds]
    counts = sum(jnp.sum(onehot, axis=0) for onehot in onehots)
    factor = rows * groups / (3.0 * counts)

    odd = plane % 2 == 1
    upper = plane // 2 == 1
    inner = (plane == 1) | (plane == 2)
    middle = [(2 * p + c, 2 * (3 - p) + c) for p in (1, 2) for c in range(2)]
    outward = [(2 * p + c, 2 * (p ^ 1) + c) for p in (1, 2) for c in range(2)]
    scaled = {}
    for k in (0, 3, 1, 2):
        mine = crossed[k]
        near = along(mine, 2)
        pair = jnp.where(odd, jnp.concatenate([near, mine]), jnp.concatenate([mine, near]))
        across = lax.ppermute(pair, "tensor", middle)
        onward = lax.ppermute(across, "tensor", outward)
        beyond = jnp.where(inner, across, onward)
        part = jnp.where(upper, jnp.concatenate([beyond, pair]), jnp.concatenate([pair, beyond]))
        other = along(part, 1)
        joined = jnp.where(
            core == 0,
            jnp.concatenate([part, other], axis=1),
            jnp.concatenate([other, part], axis=1),
        )
        token_scale = jnp.sum(onehots[k] * factor[None, :], axis=1)
        scaled[k] = (joined.astype(jnp.float32) * token_scale[:, None]).astype(jnp.bfloat16)

    def back(k, lo, hi):
        return masked_back(scaled[k][lo:hi], onehots[k][lo:hi], down_weight)

    far1 = back(3, 0, half).astype(jnp.bfloat16)
    far2 = back(3, half, rows).astype(jnp.bfloat16)
    via1, via2 = over(far1, 1), over(far2, 2)
    got1a = over(back(1, 0, half).astype(jnp.bfloat16), 1)
    got2b = over(back(2, half, rows).astype(jnp.bfloat16), 2)
    near2 = (back(2, 0, half) + via1.astype(jnp.float32)).astype(jnp.bfloat16)
    near1 = (back(1, half, rows) + via2.astype(jnp.float32)).astype(jnp.bfloat16)
    got2a = [over(near2[i * cut : (i + 1) * cut], 2) for i in range(2)]
    got1b = [over(near1[i * cut : (i + 1) * cut], 1) for i in range(2)]
    base_a = back(0, 0, half)
    base_b = back(0, half, rows)

    kinds_all = jnp.stack(kinds)[None, :, None, :]
    down_grad = None
    for picked in ((0,), (1, 2)):
        labels = jnp.array(picked, jnp.int32)[:, None, None, None]
        marks = (kinds_all == labels).astype(jnp.float32)
        down_grad = weight_grad_of(
            picked, hidden, [scaled[k] for k in range(groups)], marks, down_grad
        )

    grads = None
    for base, direct, first, got, column in (
        (base_a, got1a, 0, got2a[0], 0),
        (base_b, got2b, 0, got1b[0], half),
        (base_a, got1a, cut, got2a[1], cut),
        (base_b, got2b, cut, got1b[1], half + cut),
    ):
        grads = grads_into(base.T, direct.T, first, got.T, gate_turned, up_turned, column, grads)
    gate_grad, up_grad = grads
    return (down_grad, gate_grad.T, up_grad.T)


def shards(modality, out_grad, gate_pre, up_pre, down_weight):
    rows, block = out_grad.shape
    groups = lax.axis_size("fsdp")
    lanes = lax.axis_size("tensor")
    width = down_weight.shape[2]
    me = lax.axis_index("fsdp")
    core = lax.axis_index("tensor") % 2
    pieces = width // (2 * block)

    cores = [[i for i in range(lanes) if i % 2 == c] for c in range(2)]
    stripe = lax.all_gather(out_grad, "tensor", axis=0, axis_index_groups=cores)
    stripe = stripe.reshape(groups, pieces, rows, block)

    hidden = hidden_of(gate_pre, up_pre)
    hid_list = [hidden] + [swap(hidden, "fsdp", groups, k) for k in range(1, groups)]

    kinds = lax.all_gather(modality, "fsdp", axis=0)
    counts = jnp.sum(kind_table(kinds.reshape(-1)), axis=0)
    factor = rows * groups / (3.0 * counts)

    order = [groups - 1] + list(range(1, groups - 1)) + [0]
    onehots, scaled = {}, {}
    for k in order:
        part = lax.dynamic_index_in_dim(stripe, me ^ k, 0, keepdims=False)
        if k:
            part = swap(part, "fsdp", groups, k)
        other = swap(part, "tensor", lanes, 1)
        first = jnp.where(core == 0, part, other)
        second = jnp.where(core == 0, other, part)
        joined = jnp.stack([first, second], axis=1).reshape(2 * pieces, rows, block)
        joined = jnp.concatenate([joined[i] for i in range(2 * pieces)], axis=1)
        onehots[k] = kind_table(lax.dynamic_index_in_dim(kinds, me ^ k, 0, keepdims=False))
        token_scale = jnp.sum(onehots[k] * factor[None, :], axis=1)
        scaled[k] = (joined.astype(jnp.float32) * token_scale[:, None]).astype(jnp.bfloat16)

    folded = masked_back(scaled[0], onehots[0], down_weight)
    for k in range(1, groups):
        sent = masked_back(scaled[k], onehots[k], down_weight).astype(jnp.bfloat16)
        folded = folded + swap(sent, "fsdp", groups, k).astype(jnp.float32)
    gate_grad, up_grad = grads_of(folded, gate_pre, up_pre)

    hid_all = jnp.concatenate(hid_list, axis=0)
    scaled_all = jnp.concatenate([scaled[k] for k in range(groups)], axis=0)
    onehot_all = jnp.concatenate([onehots[k] for k in range(groups)], axis=0)
    down_grad = weight_grad(hid_all, scaled_all, onehot_all)
    return (down_grad, gate_grad, up_grad)


def solution(mesh):
    placed = (
        P("fsdp"),
        P("fsdp", "tensor"),
        P("fsdp", "tensor"),
        P("fsdp", "tensor"),
        P(None, "tensor", "fsdp"),
    )
    square = mesh.shape["fsdp"] == 4 and mesh.shape["tensor"] == 8
    return jax.shard_map(
        shards_planes if square else shards,
        mesh=mesh,
        in_specs=placed,
        out_specs=(P(None, "tensor", "fsdp"), P("fsdp", "tensor"), P("fsdp", "tensor")),
        check_vma=False,
    )
```

profile of v0, /device:TPU:8, one launch (start us, length us, event | category | flops | bytes accessed | tf_op | source)
XLA Modules:
  0.0 297.1 jit_solution(17836506511992299898)
XLA Ops:
  0.6 2.5 collective-permute-start.15
  4.2 3.5 %fusion.28 = (bf16[1376,512]{1,0:T(8,128)(2,1)S(1)}, bf16[1376,512]{1,0:T(8,128)(2,1)S(1)}) fusion(bf16[1376,1024]{1,0:T(8,128)(2,1)} %bitcast.92, bf16[1376,1024]{1,0:T(8,128)(2,1)} %bitcast.97), kind=kLoop, calls=%fused_computation.38 | loop fusion | flops 11272192 | bytes 8454144 | tf_op jit(solution)/shard_map/convert_element_type | solution.py:29
  15.9 15.1 %collective-permute-done.8 = bf16[256,512]{1,0:T(8,128)(2,1)} collective-permute-done((bf16[256,512]{1,0:T(8,128)(2,1)}, bf16[256,512]{1,0:T(8,128)(2,1)}, u32[]{:S(2)}, u32[]{:S(2)}) %collective-permute-start.8) | collective-permute-done | bytes 262176 | tf_op jit(solution)/shard_map/ppermute | solution.py:236
  30.9 3.6 %collective-permute-done.7 = bf16[256,512]{1,0:T(8,128)(2,1)S(1)} collective-permute-done((bf16[256,512]{1,0:T(8,128)(2,1)}, bf16[256,512]{1,0:T(8,128)(2,1)S(1)}, u32[]{:S(2)}, u32[]{:S(2)}) %collective-permute-start.7) | collective-permute-done | bytes 262176 | tf_op jit(solution)/shard_map/ppermute | solution.py:236
  35.7 2.3 collective-permute-start.9
  41.9 5.3 %collective-permute-done.16 = bf16[256,512]{1,0:T(8,128)(2,1)S(1)} collective-permute-done((bf16[256,512]{1,0:T(8,128)(2,1)S(1)}, bf16[256,512]{1,0:T(8,128)(2,1)S(1)}, u32[]{:S(2)}, u32[]{:S(2)}) %collective-permute-start.16) | collective-permute-done | bytes 262176 | tf_op jit(solution)/shard_map/ppermute | solution.py:233
  47.5 4.9 %collective-permute-start.10 = (bf16[512,512]{1,0:T(8,128)(2,1)S(1)}, bf16[512,512]{1,0:T(8,128)(2,1)S(1)}, u32[]{:S(2)}, u32[]{:S(2)}) collective-permute-start(bf16[512,512]{1,0:T(8,128)(2,1)S(1)} %maximum_select_fusion.8), channel_id=1, source_target_pairs={{2,4},{3,5},{4,2},{5,3},{10,12},{11,13},{12,10},{13,11},{18,20},{1... | collective-permute-start | bytes 1572872 | tf_op jit(solution)/shard_map/ppermute | solution.py:273
  56.6 3.5 %collective-permute-start.18 = (bf16[512,512]{1,0:T(8,128)(2,1)S(1)}, bf16[512,512]{1,0:T(8,128)(2,1)S(1)}, u32[]{:S(2)}, u32[]{:S(2)}) collective-permute-start(bf16[512,512]{1,0:T(8,128)(2,1)S(1)} %maximum_select_fusion.9), channel_id=1, source_target_pairs={{2,4},{3,5},{4,2},{5,3},{10,12},{11,13},{12,10},{13,11},{18,20},{1... | collective-permute-start | bytes 1572872 | tf_op jit(solution)/shard_map/ppermute | solution.py:273
  65.0 3.3 %collective-permute-start.28 = (bf16[512,512]{1,0:T(8,128)(2,1)S(1)}, bf16[512,512]{1,0:T(8,128)(2,1)S(1)}, u32[]{:S(2)}, u32[]{:S(2)}) collective-permute-start(bf16[512,512]{1,0:T(8,128)(2,1)S(1)} %maximum_select_fusion.11), channel_id=1, source_target_pairs={{2,4},{3,5},{4,2},{5,3},{10,12},{11,13},{12,10},{13,11},{18,20},{1... | collective-permute-start | bytes 1572872 | tf_op jit(solution)/shard_map/ppermute | solution.py:273
  69.7 6.5 %collective-permute-done.18 = bf16[512,512]{1,0:T(8,128)(2,1)S(1)} collective-permute-done((bf16[512,512]{1,0:T(8,128)(2,1)S(1)}, bf16[512,512]{1,0:T(8,128)(2,1)S(1)}, u32[]{:S(2)}, u32[]{:S(2)}) %collective-permute-start.18) | collective-permute-done | bytes 524320 | tf_op jit(solution)/shard_map/ppermute | solution.py:273
  77.7 9.8 %collective-permute-done.23 = bf16[512,512]{1,0:T(8,128)(2,1)S(1)} collective-permute-done((bf16[512,512]{1,0:T(8,128)(2,1)S(1)}, bf16[512,512]{1,0:T(8,128)(2,1)S(1)}, u32[]{:S(2)}, u32[]{:S(2)}) %collective-permute-start.23) | collective-permute-done | bytes 524320 | tf_op jit(solution)/shard_map/ppermute | solution.py:273
  89.2 4.9 %collective-permute-done.28 = bf16[512,512]{1,0:T(8,128)(2,1)S(1)} collective-permute-done((bf16[512,512]{1,0:T(8,128)(2,1)S(1)}, bf16[512,512]{1,0:T(8,128)(2,1)S(1)}, u32[]{:S(2)}, u32[]{:S(2)}) %collective-permute-start.28) | collective-permute-done | bytes 524320 | tf_op jit(solution)/shard_map/ppermute | solution.py:273
  98.5 9.2 %collective-permute-done.24 = bf16[512,512]{1,0:T(8,128)(2,1)S(1)} collective-permute-done((bf16[512,512]{1,0:T(8,128)(2,1)S(1)}, bf16[512,512]{1,0:T(8,128)(2,1)S(1)}, u32[]{:S(2)}, u32[]{:S(2)}) %collective-permute-start.24) | collective-permute-done | bytes 524320 | tf_op jit(solution)/shard_map/ppermute | solution.py:274
  109.7 4.0 %collective-permute-done.29 = bf16[512,512]{1,0:T(8,128)(2,1)S(1)} collective-permute-done((bf16[512,512]{1,0:T(8,128)(2,1)S(1)}, bf16[512,512]{1,0:T(8,128)(2,1)S(1)}, u32[]{:S(2)}, u32[]{:S(2)}) %collective-permute-start.29) | collective-permute-done | bytes 524320 | tf_op jit(solution)/shard_map/ppermute | solution.py:274
  116.1 4.9 %convolution_bitcast_fusion.7.base_ref = f32[1376,512]{1,0:T(8,128)S(1)} fusion(bf16[3,1376,1024]{2,1,0:T(8,128)(2,1)S(1)} %bitcast.124, bf16[3,512]{1,0:T(4,128)(2,1)S(1)} %get-tuple-element.52, bf16[512,1024]{1,0:T(8,128)(2,1)S(1)} %get-tuple-element.32), kind=kOutput, calls=%fused_computation.15 | convolution fusion | flops 4330094592 | bytes 12323840 | tf_op jit(solution)/shard_map/dot_general | solution.py:43
  121.0 4.8 %convolution_bitcast_fusion.3.base_ref = f32[1376,512]{1,0:T(8,128)S(1)} fusion(bf16[3,1376,1024]{2,1,0:T(8,128)(2,1)S(1)} %bitcast.124, bf16[3,512]{1,0:T(4,128)(2,1)S(1)} %get-tuple-element.51, bf16[512,1024]{1,0:T(8,128)(2,1)S(1)} %get-tuple-element.31), kind=kOutput, calls=%fused_computation.11 | convolution fusion | flops 4330094592 | bytes 12323840 | tf_op jit(solution)/shard_map/dot_general | solution.py:43
  125.8 8.3 %collective-permute-done.1.refs_3_ = bf16[1376,512]{1,0:T(8,128)(2,1)S(1)} collective-permute-done((bf16[1376,512]{1,0:T(8,128)(2,1)S(1)}, bf16[1376,512]{1,0:T(8,128)(2,1)S(1)}, u32[]{:S(2)}, u32[]{:S(2)}) %collective-permute-start.1) | collective-permute-done | bytes 1409056 | tf_op jit(solution)/shard_map/ppermute | solution.py:233
  134.1 2.4 collective-permute-start.3
  140.7 8.1 %fusion.11 = bf16[512,1376]{0,1:T(8,128)(2,1)S(1)} fusion(bf16[3,1376,1024]{2,1,0:T(8,128)(2,1)} %param.11, bf16[3,512]{1,0:T(4,128)(2,1)S(1)} %get-tuple-element.48, bf16[512,1024]{1,0:T(8,128)(2,1)S(1)} %get-tuple-element.28), kind=kOutput, calls=%fused_computation.25 | convolution fusion | flops 4330799104 | bytes 10914816 | tf_op jit(solution)/shard_map/dot_general | solution.py:43
  152.1 8.1 %fusion.8 = bf16[512,1376]{0,1:T(8,128)(2,1)S(1)} fusion(bf16[3,1376,1024]{2,1,0:T(8,128)(2,1)} %param.11, bf16[3,512]{1,0:T(4,128)(2,1)S(1)} %get-tuple-element.46, bf16[512,1024]{1,0:T(8,128)(2,1)S(1)} %get-tuple-element.26), kind=kOutput, calls=%fused_computation.24 | convolution fusion | flops 4330799104 | bytes 10914816 | tf_op jit(solution)/shard_map/dot_general | solution.py:43
  160.2 9.4 %fusion.14 = bf16[512,1376]{0,1:T(8,128)(2,1)} fusion(bf16[3,1376,1024]{2,1,0:T(8,128)(2,1)} %param.11, bf16[3,512]{1,0:T(4,128)(2,1)S(1)} %get-tuple-element.49, bf16[512,1024]{1,0:T(8,128)(2,1)S(1)} %get-tuple-element.29), kind=kOutput, calls=%fused_computation.26 | convolution fusion | flops 4330799104 | bytes 10914816 | tf_op jit(solution)/shard_map/dot_general | solution.py:43
  169.7 8.1 %fusion.17 = bf16[512,1376]{0,1:T(8,128)(2,1)S(1)} fusion(bf16[3,1376,1024]{2,1,0:T(8,128)(2,1)} %param.11, bf16[3,512]{1,0:T(4,128)(2,1)S(1)} %get-tuple-element.47, bf16[512,1024]{1,0:T(8,128)(2,1)S(1)} %get-tuple-element.27), kind=kOutput, calls=%fused_computation.27 | convolution fusion | flops 4330799104 | bytes 10914816 | tf_op jit(solution)/shard_map/dot_general | solution.py:43
  180.0 18.4 %collective-permute-done.5.refs_7_ = bf16[1376,512]{1,0:T(8,128)(2,1)S(1)} collective-permute-done((bf16[1376,512]{1,0:T(8,128)(2,1)S(1)}, bf16[1376,512]{1,0:T(8,128)(2,1)S(1)}, u32[]{:S(2)}, u32[]{:S(2)}) %collective-permute-start.5) | collective-permute-done | bytes 1409056 | tf_op jit(solution)/shard_map/ppermute | solution.py:233
  198.4 17.7 %shard_map.94.refs_13_ = f32[3,1376,1024]{2,1,0:T(8,128)} custom-call(bf16[1376,512]{1,0:T(8,128)(2,1)S(1)} %get-tuple-element.24.refs_0_, bf16[1376,512]{1,0:T(8,128)(2,1)S(1)} %get-tuple-element.23.refs_1_, bf16[1376,512]{1,0:T(8,128)(2,1)} %collective-permute-done.refs_2_, bf16[1376,512]{1,0:T(8,128)(2,1)S(1)} %collective-permute-done.1.refs_3_, ...), custom_call_target="tpu_custom_call" | custom-call | flops 11542724608 | bytes 25296896 | tf_op jit(solution)/shard_map/pallas_call | solution.py:146
  216.1 12.5 %collective-permute-done.32 = bf16[512,1376]{0,1:T(8,128)(2,1)S(1)} collective-permute-done((bf16[512,1376]{0,1:T(8,128)(2,1)S(1)}, bf16[512,1376]{0,1:T(8,128)(2,1)S(1)}, u32[]{:S(2)}, u32[]{:S(2)}) %collective-permute-start.32) | collective-permute-done | bytes 1409056 | tf_op jit(solution)/shard_map/ppermute | solution.py:233
  228.6 8.1 %add_convert_fusion.1 = bf16[512,1376]{0,1:T(8,128)(2,1)S(1)} fusion(bf16[512,1376]{0,1:T(8,128)(2,1)S(1)} %collective-permute-done.32, bf16[3,1376,1024]{2,1,0:T(8,128)(2,1)} %param.11, bf16[3,512]{1,0:T(4,128)(2,1)S(1)} %get-tuple-element.50, bf16[512,1024]{1,0:T(8,128)(2,1)S(1)} %get-tuple-element.30), kind=kOutput, calls=%fused_computation.37 | convolution fusion | flops 4332208128 | bytes 12323840 | tf_op jit(solution)/shard_map/dot_general | solution.py:43
  238.4 3.9 %collective-permute-done.35 = bf16[512,1376]{0,1:T(8,128)(2,1)} collective-permute-done((bf16[512,1376]{0,1:T(8,128)(2,1)S(1)}, bf16[512,1376]{0,1:T(8,128)(2,1)}, u32[]{:S(2)}, u32[]{:S(2)}) %collective-permute-start.35) | collective-permute-done | bytes 1409056 | tf_op jit(solution)/shard_map/ppermute | solution.py:233
  242.3 9.0 %add_convert_fusion = bf16[512,1376]{0,1:T(8,128)(2,1)S(1)} fusion(bf16[512,1376]{0,1:T(8,128)(2,1)} %collective-permute-done.35, bf16[3,1376,1024]{2,1,0:T(8,128)(2,1)} %param.11, bf16[3,512]{1,0:T(4,128)(2,1)S(1)} %get-tuple-element.45, bf16[512,1024]{1,0:T(8,128)(2,1)S(1)} %get-tuple-element.25), kind=kOutput, calls=%fused_computation.36 | convolution fusion | flops 4332208128 | bytes 12323840 | tf_op jit(solution)/shard_map/dot_general | solution.py:43
  254.0 33.9 %shard_map.95 = f32[3,1376,1024]{2,1,0:T(8,128)} custom-call(bf16[1376,512]{1,0:T(8,128)(2,1)S(1)} %get-tuple-element.24.refs_0_, bf16[1376,512]{1,0:T(8,128)(2,1)S(1)} %get-tuple-element.23.refs_1_, bf16[1376,512]{1,0:T(8,128)(2,1)} %collective-permute-done.refs_2_, ...), custom_call_target="tpu_custom_call", output_to_operand_aliasing={{}: (13, {})} | custom-call | flops 23085449216 | bytes 30932992 | tf_op jit(solution)/shard_map/pallas_call | solution.py:146
  287.9 2.2 shard_map.96
  290.1 2.2 shard_map.97
  292.4 2.2 shard_map.98
  (122 shorter events, 52.9 us)
Async XLA Ops:
  0.6 13.8 %collective-permute-start.15 = (s32[1024]{0:T(1024)}, s32[1024]{0:T(1024)S(1)}, u32[]{:S(2)}, u32[]{:S(2)}) collective-permute-start(s32[1024]{0:T(1024)} %param.7), channel_id=1, source_target_pairs={{0,24},{8,16},{16,8},{24,0},{1,25},{9,17},{17,9},{25,1},{2,26},{10... | collective-permute-start | bytes 12296 | tf_op jit(solution)/shard_map/ppermute | solution.py:233
  7.7 170.1 %collective-permute-start = (bf16[1376,512]{1,0:T(8,128)(2,1)S(1)}, bf16[1376,512]{1,0:T(8,128)(2,1)}, u32[]{:S(2)}, u32[]{:S(2)}) collective-permute-start(bf16[1376,512]{1,0:T(8,128)(2,1)S(1)} %get-tuple-element.24.refs_0_), channel_id=1, source_target_pairs={{0,8},{8,0},{16,24},{24,16},{1,9},{9,1},{17,25},{25,17},{2,10},{10... | collective-permute-start | bytes 4227080 | tf_op jit(solution)/shard_map/ppermute | solution.py:233
  11.3 19.6 %collective-permute-start.8 = (bf16[256,512]{1,0:T(8,128)(2,1)}, bf16[256,512]{1,0:T(8,128)(2,1)}, u32[]{:S(2)}, u32[]{:S(2)}) collective-permute-start(bf16[256,512]{1,0:T(8,128)(2,1)} %get-tuple-element.42), channel_id=1, source_target_pairs={{0,6},{1,7},{2,4},{3,5},{4,2},{5,3},{6,0},{7,1},{8,14},{9,15},{10,... | collective-permute-start | bytes 786440 | tf_op jit(solution)/shard_map/ppermute | solution.py:236
  13.1 21.4 %collective-permute-start.7 = (bf16[256,512]{1,0:T(8,128)(2,1)}, bf16[256,512]{1,0:T(8,128)(2,1)S(1)}, u32[]{:S(2)}, u32[]{:S(2)}) collective-permute-start(bf16[256,512]{1,0:T(8,128)(2,1)} %get-tuple-element.43), channel_id=1, source_target_pairs={{0,4},{1,5},{2,6},{3,7},{4,0},{5,1},{6,2},{7,3},{8,12},{9,13},{10,... | collective-permute-start | bytes 786440 | tf_op jit(solution)/shard_map/ppermute | solution.py:236
  14.5 20.1 %collective-permute-start.6 = (bf16[256,512]{1,0:T(8,128)(2,1)S(1)}, bf16[256,512]{1,0:T(8,128)(2,1)S(1)}, u32[]{:S(2)}, u32[]{:S(2)}) collective-permute-start(bf16[256,512]{1,0:T(8,128)(2,1)S(1)} %get-tuple-element.44), channel_id=1, source_target_pairs={{0,2},{1,3},{2,0},{3,1},{4,6},{5,7},{6,4},{7,5},{8,10},{9,11},{10,... | collective-permute-start | bytes 786440 | tf_op jit(solution)/shard_map/ppermute | solution.py:236
  38.7 13.8 %collective-permute-start.21 = (bf16[256,512]{1,0:T(8,128)(2,1)S(1)}, bf16[256,512]{1,0:T(8,128)(2,1)S(1)}, u32[]{:S(2)}, u32[]{:S(2)}) collective-permute-start(bf16[256,512]{1,0:T(8,128)(2,1)S(1)} %get-tuple-element.38), channel_id=1, source_target_pairs={{0,16},{8,24},{16,0},{24,8},{1,17},{9,25},{17,1},{25,9},{2,18},{10... | collective-permute-start | bytes 786440 | tf_op jit(solution)/shard_map/ppermute | solution.py:233
  40.3 12.3 %collective-permute-start.26 = (bf16[256,512]{1,0:T(8,128)(2,1)S(1)}, bf16[256,512]{1,0:T(8,128)(2,1)S(1)}, u32[]{:S(2)}, u32[]{:S(2)}) collective-permute-start(bf16[256,512]{1,0:T(8,128)(2,1)S(1)} %get-tuple-element.37), channel_id=1, source_target_pairs={{0,24},{8,16},{16,8},{24,0},{1,25},{9,17},{17,9},{25,1},{2,26},{10... | collective-permute-start | bytes 786440 | tf_op jit(solution)/shard_map/ppermute | solution.py:233
  47.5 20.8 %collective-permute-start.10 = (bf16[512,512]{1,0:T(8,128)(2,1)S(1)}, bf16[512,512]{1,0:T(8,128)(2,1)S(1)}, u32[]{:S(2)}, u32[]{:S(2)}) collective-permute-start(bf16[512,512]{1,0:T(8,128)(2,1)S(1)} %maximum_select_fusion.8), channel_id=1, source_target_pairs={{2,4},{3,5},{4,2},{5,3},{10,12},{11,13},{12,10},{13,11},{18,20},{1... | collective-permute-start | bytes 1572872 | tf_op jit(solution)/shard_map/ppermute | solution.py:273
  52.6 12.2 %collective-permute-start.27 = (bf16[256,512]{1,0:T(8,128)(2,1)S(1)}, bf16[256,512]{1,0:T(8,128)(2,1)S(1)}, u32[]{:S(2)}, u32[]{:S(2)}) collective-permute-start(bf16[256,512]{1,0:T(8,128)(2,1)S(1)} %collective-permute-done.26), channel_id=1, source_target_pairs={{0,2},{1,3},{2,0},{3,1},{4,6},{5,7},{6,4},{7,5},{8,10},{9,11},{10,... | collective-permute-start | bytes 786440 | tf_op jit(solution)/shard_map/ppermute | solution.py:236
  56.6 19.7 %collective-permute-start.18 = (bf16[512,512]{1,0:T(8,128)(2,1)S(1)}, bf16[512,512]{1,0:T(8,128)(2,1)S(1)}, u32[]{:S(2)}, u32[]{:S(2)}) collective-permute-start(bf16[512,512]{1,0:T(8,128)(2,1)S(1)} %maximum_select_fusion.9), channel_id=1, source_target_pairs={{2,4},{3,5},{4,2},{5,3},{10,12},{11,13},{12,10},{13,11},{18,20},{1... | collective-permute-start | bytes 1572872 | tf_op jit(solution)/shard_map/ppermute | solution.py:273
  62.2 25.3 %collective-permute-start.23 = (bf16[512,512]{1,0:T(8,128)(2,1)S(1)}, bf16[512,512]{1,0:T(8,128)(2,1)S(1)}, u32[]{:S(2)}, u32[]{:S(2)}) collective-permute-start(bf16[512,512]{1,0:T(8,128)(2,1)S(1)} %maximum_select_fusion.10), channel_id=1, source_target_pairs={{2,4},{3,5},{4,2},{5,3},{10,12},{11,13},{12,10},{13,11},{18,20},{1... | collective-permute-start | bytes 1572872 | tf_op jit(solution)/shard_map/ppermute | solution.py:273
  65.0 29.1 %collective-permute-start.28 = (bf16[512,512]{1,0:T(8,128)(2,1)S(1)}, bf16[512,512]{1,0:T(8,128)(2,1)S(1)}, u32[]{:S(2)}, u32[]{:S(2)}) collective-permute-start(bf16[512,512]{1,0:T(8,128)(2,1)S(1)} %maximum_select_fusion.11), channel_id=1, source_target_pairs={{2,4},{3,5},{4,2},{5,3},{10,12},{11,13},{12,10},{13,11},{18,20},{1... | collective-permute-start | bytes 1572872 | tf_op jit(solution)/shard_map/ppermute | solution.py:273
  68.3 27.2 %collective-permute-start.11 = (bf16[512,512]{1,0:T(8,128)(2,1)S(1)}, bf16[512,512]{1,0:T(8,128)(2,1)S(1)}, u32[]{:S(2)}, u32[]{:S(2)}) collective-permute-start(bf16[512,512]{1,0:T(8,128)(2,1)S(1)} %collective-permute-done.10), channel_id=1, source_target_pairs={{2,0},{3,1},{4,6},{5,7},{10,8},{11,9},{12,14},{13,15},{18,16},{19,... | collective-permute-start | bytes 1572872 | tf_op jit(solution)/shard_map/ppermute | solution.py:274
  76.3 21.6 %collective-permute-start.19 = (bf16[512,512]{1,0:T(8,128)(2,1)S(1)}, bf16[512,512]{1,0:T(8,128)(2,1)S(1)}, u32[]{:S(2)}, u32[]{:S(2)}) collective-permute-start(bf16[512,512]{1,0:T(8,128)(2,1)S(1)} %collective-permute-done.18), channel_id=1, source_target_pairs={{2,0},{3,1},{4,6},{5,7},{10,8},{11,9},{12,14},{13,15},{18,16},{19,... | collective-permute-start | bytes 1572872 | tf_op jit(solution)/shard_map/ppermute | solution.py:274
  87.5 49.0 %collective-permute-start.2 = (bf16[1376,512]{1,0:T(8,128)(2,1)S(1)}, bf16[1376,512]{1,0:T(8,128)(2,1)S(1)}, u32[]{:S(2)}, u32[]{:S(2)}) collective-permute-start(bf16[1376,512]{1,0:T(8,128)(2,1)S(1)} %get-tuple-element.24.refs_0_), channel_id=1, source_target_pairs={{0,16},{8,24},{16,0},{24,8},{1,17},{9,25},{17,1},{25,9},{2,18},{10... | collective-permute-start | bytes 4227080 | tf_op jit(solution)/shard_map/ppermute | solution.py:233
  94.1 13.6 %collective-permute-start.24 = (bf16[512,512]{1,0:T(8,128)(2,1)S(1)}, bf16[512,512]{1,0:T(8,128)(2,1)S(1)}, u32[]{:S(2)}, u32[]{:S(2)}) collective-permute-start(bf16[512,512]{1,0:T(8,128)(2,1)S(1)} %collective-permute-done.23), channel_id=1, source_target_pairs={{2,0},{3,1},{4,6},{5,7},{10,8},{11,9},{12,14},{13,15},{18,16},{19,... | collective-permute-start | bytes 1572872 | tf_op jit(solution)/shard_map/ppermute | solution.py:274
  95.4 18.3 %collective-permute-start.29 = (bf16[512,512]{1,0:T(8,128)(2,1)S(1)}, bf16[512,512]{1,0:T(8,128)(2,1)S(1)}, u32[]{:S(2)}, u32[]{:S(2)}) collective-permute-start(bf16[512,512]{1,0:T(8,128)(2,1)S(1)} %collective-permute-done.28), channel_id=1, source_target_pairs={{2,0},{3,1},{4,6},{5,7},{10,8},{11,9},{12,14},{13,15},{18,16},{19,... | collective-permute-start | bytes 1572872 | tf_op jit(solution)/shard_map/ppermute | solution.py:274
  97.9 16.4 %collective-permute-start.12 = (bf16[1024,512]{1,0:T(8,128)(2,1)S(1)}, bf16[1024,512]{1,0:T(8,128)(2,1)S(1)}, u32[]{:S(2)}, u32[]{:S(2)}) collective-permute-start(bf16[1024,512]{1,0:T(8,128)(2,1)S(1)} %maximum_select_fusion.4), channel_id=1, source_target_pairs={{0,1},{1,0},{2,3},{3,2},{4,5},{5,4},{6,7},{7,6},{8,9},{9,8},{10,11... | collective-permute-start | bytes 3145736 | tf_op jit(solution)/shard_map/ppermute | solution.py:236
  107.7 26.4 %collective-permute-start.1 = (bf16[1376,512]{1,0:T(8,128)(2,1)S(1)}, bf16[1376,512]{1,0:T(8,128)(2,1)S(1)}, u32[]{:S(2)}, u32[]{:S(2)}) collective-permute-start(bf16[1376,512]{1,0:T(8,128)(2,1)S(1)} %get-tuple-element.23.refs_1_), channel_id=1, source_target_pairs={{0,8},{8,0},{16,24},{24,16},{1,9},{9,1},{17,25},{25,17},{2,10},{10... | collective-permute-start | bytes 4227080 | tf_op jit(solution)/shard_map/ppermute | solution.py:233
  113.7 24.2 %collective-permute-start.25 = (bf16[1024,512]{1,0:T(8,128)(2,1)S(1)}, bf16[1024,512]{1,0:T(8,128)(2,1)S(1)}, u32[]{:S(2)}, u32[]{:S(2)}) collective-permute-start(bf16[1024,512]{1,0:T(8,128)(2,1)S(1)} %maximum_select_fusion.6), channel_id=1, source_target_pairs={{0,1},{1,0},{2,3},{3,2},{4,5},{5,4},{6,7},{7,6},{8,9},{9,8},{10,11... | collective-permute-start | bytes 3145736 | tf_op jit(solution)/shard_map/ppermute | solution.py:236
  114.3 24.9 %collective-permute-start.30 = (bf16[1024,512]{1,0:T(8,128)(2,1)S(1)}, bf16[1024,512]{1,0:T(8,128)(2,1)S(1)}, u32[]{:S(2)}, u32[]{:S(2)}) collective-permute-start(bf16[1024,512]{1,0:T(8,128)(2,1)S(1)} %maximum_select_fusion.7), channel_id=1, source_target_pairs={{0,1},{1,0},{2,3},{3,2},{4,5},{5,4},{6,7},{7,6},{8,9},{9,8},{10,11... | collective-permute-start | bytes 3145736 | tf_op jit(solution)/shard_map/ppermute | solution.py:236
  134.1 43.8 %collective-permute-start.3 = (bf16[1376,512]{1,0:T(8,128)(2,1)S(1)}, bf16[1376,512]{1,0:T(8,128)(2,1)S(1)}, u32[]{:S(2)}, u32[]{:S(2)}) collective-permute-start(bf16[1376,512]{1,0:T(8,128)(2,1)S(1)} %get-tuple-element.23.refs_1_), channel_id=1, source_target_pairs={{0,16},{8,24},{16,0},{24,8},{1,17},{9,25},{17,1},{25,9},{2,18},{10... | collective-permute-start | bytes 4227080 | tf_op jit(solution)/shard_map/ppermute | solution.py:233
  136.5 42.1 %collective-permute-start.4 = (bf16[1376,512]{1,0:T(8,128)(2,1)S(1)}, bf16[1376,512]{1,0:T(8,128)(2,1)S(1)}, u32[]{:S(2)}, u32[]{:S(2)}) collective-permute-start(bf16[1376,512]{1,0:T(8,128)(2,1)S(1)} %collective-permute-done.2.refs_4_), channel_id=1, source_target_pairs={{0,8},{8,0},{16,24},{24,16},{1,9},{9,1},{17,25},{25,17},{2,10},{10... | collective-permute-start | bytes 4227080 | tf_op jit(solution)/shard_map/ppermute | solution.py:233
  138.0 60.4 %collective-permute-start.5 = (bf16[1376,512]{1,0:T(8,128)(2,1)S(1)}, bf16[1376,512]{1,0:T(8,128)(2,1)S(1)}, u32[]{:S(2)}, u32[]{:S(2)}) collective-permute-start(bf16[1376,512]{1,0:T(8,128)(2,1)S(1)} %collective-permute-done.1.refs_3_), channel_id=1, source_target_pairs={{0,16},{8,24},{16,0},{24,8},{1,17},{9,25},{17,1},{25,9},{2,18},{10... | collective-permute-start | bytes 4227080 | tf_op jit(solution)/shard_map/ppermute | solution.py:233
  148.8 79.8 %collective-permute-start.32 = (bf16[512,1376]{0,1:T(8,128)(2,1)S(1)}, bf16[512,1376]{0,1:T(8,128)(2,1)S(1)}, u32[]{:S(2)}, u32[]{:S(2)}) collective-permute-start(bf16[512,1376]{0,1:T(8,128)(2,1)S(1)} %fusion.11), channel_id=1, source_target_pairs={{0,16},{8,24},{16,0},{24,8},{1,17},{9,25},{17,1},{25,9},{2,18},{10... | collective-permute-start | bytes 4227080 | tf_op jit(solution)/shard_map/ppermute | solution.py:233
  177.8 112.3 %collective-permute-start.31 = (bf16[512,1376]{0,1:T(8,128)(2,1)S(1)}, bf16[512,1376]{0,1:T(8,128)(2,1)S(1)}, u32[]{:S(2)}, u32[]{:S(2)}) collective-permute-start(bf16[512,1376]{0,1:T(8,128)(2,1)S(1)} %fusion.8), channel_id=1, source_target_pairs={{0,16},{8,24},{16,0},{24,8},{1,17},{9,25},{17,1},{25,9},{2,18},{10... | collective-permute-start | bytes 4227080 | tf_op jit(solution)/shard_map/ppermute | solution.py:233
  177.9 75.9 %collective-permute-start.34 = (bf16[512,1376]{0,1:T(8,128)(2,1)}, bf16[512,1376]{0,1:T(8,128)(2,1)S(1)}, u32[]{:S(2)}, u32[]{:S(2)}) collective-permute-start(bf16[512,1376]{0,1:T(8,128)(2,1)} %fusion.14), channel_id=1, source_target_pairs={{0,8},{8,0},{16,24},{24,16},{1,9},{9,1},{17,25},{25,17},{2,10},{10... | collective-permute-start | bytes 4227080 | tf_op jit(solution)/shard_map/ppermute | solution.py:233
  178.5 63.7 %collective-permute-start.35 = (bf16[512,1376]{0,1:T(8,128)(2,1)S(1)}, bf16[512,1376]{0,1:T(8,128)(2,1)}, u32[]{:S(2)}, u32[]{:S(2)}) collective-permute-start(bf16[512,1376]{0,1:T(8,128)(2,1)S(1)} %fusion.17), channel_id=1, source_target_pairs={{0,8},{8,0},{16,24},{24,16},{1,9},{9,1},{17,25},{25,17},{2,10},{10... | collective-permute-start | bytes 4227080 | tf_op jit(solution)/shard_map/ppermute | solution.py:233
  236.8 57.8 %collective-permute-start.33 = (bf16[256,1376]{0,1:T(8,128)(2,1)S(1)}, bf16[256,1376]{0,1:T(8,128)(2,1)S(1)}, u32[]{:S(2)}, u32[]{:S(2)}) collective-permute-start(bf16[256,1376]{0,1:T(8,128)(2,1)S(1)} %get-tuple-element.36), channel_id=1, source_target_pairs={{0,8},{8,0},{16,24},{24,16},{1,9},{9,1},{17,25},{25,17},{2,10},{10... | collective-permute-start | bytes 2113544 | tf_op jit(solution)/shard_map/ppermute | solution.py:233
  251.3 41.0 %collective-permute-start.36 = (bf16[256,1376]{0,1:T(8,128)(2,1)S(1)}, bf16[256,1376]{0,1:T(8,128)(2,1)S(1)}, u32[]{:S(2)}, u32[]{:S(2)}) collective-permute-start(bf16[256,1376]{0,1:T(8,128)(2,1)S(1)} %get-tuple-element.34), channel_id=1, source_target_pairs={{0,16},{8,24},{16,0},{24,8},{1,17},{9,25},{17,1},{25,9},{2,18},{10... | collective-permute-start | bytes 2113544 | tf_op jit(solution)/shard_map/ppermute | solution.py:233
  253.3 36.8 %collective-permute-start.37 = (bf16[256,1376]{0,1:T(8,128)(2,1)S(1)}, bf16[256,1376]{0,1:T(8,128)(2,1)S(1)}, u32[]{:S(2)}, u32[]{:S(2)}) collective-permute-start(bf16[256,1376]{0,1:T(8,128)(2,1)S(1)} %get-tuple-element.35), channel_id=1, source_target_pairs={{0,8},{8,0},{16,24},{24,16},{1,9},{9,1},{17,25},{25,17},{2,10},{10... | collective-permute-start | bytes 2113544 | tf_op jit(solution)/shard_map/ppermute | solution.py:233
  253.9 34.0 %collective-permute-start.38 = (bf16[256,1376]{0,1:T(8,128)(2,1)S(1)}, bf16[256,1376]{0,1:T(8,128)(2,1)S(1)}, u32[]{:S(2)}, u32[]{:S(2)}) collective-permute-start(bf16[256,1376]{0,1:T(8,128)(2,1)S(1)} %get-tuple-element.33), channel_id=1, source_target_pairs={{0,16},{8,24},{16,0},{24,8},{1,17},{9,25},{17,1},{25,9},{2,18},{10... | collective-permute-start | bytes 2113544 | tf_op jit(solution)/shard_map/ppermute | solution.py:233
  (16 other events, 251.2 us)
where the time goes:
time: 302 us; the launch traced here: 297 us
  waiting for transfers between devices  106 us (35%)
  matrix products  60.5 us (20%)
  Pallas kernels  60.5 us (20%)
  starting transfers between devices  53.2 us (18%)
  other arithmetic  12.7 us (4%)
  local copies, waits for them, and re-layouts  3.07 us (1%)
    dot_general x8, matrix products, masked_back(): lax.dot_general(masked, down_weight, (((0, 2), (0, 2)), ((), ())), prefer...  60.5 us
    pallas_call x2, Pallas kernels, weight_grad_of(): pl.pallas_call(functools.partial(weight_body, kinds, tuple(owners), cols...  51.6 us
    ppermute x20, waiting for transfers between devices, over(): return lax.ppermute(values, 'fsdp', [(i, i ^ step) for i in range(groups)])  48.4 us
    ppermute x20, starting transfers between devices, over(): return lax.ppermute(values, 'fsdp', [(i, i ^ step) for i in range(groups)])  24.1 us
    ppermute x11, waiting for transfers between devices, along(): return lax.ppermute(values, 'tensor', [(i, i ^ step) for i in range(lanes)])  22.7 us
    ppermute x4, waiting for transfers between devices, planes_body(): across = lax.ppermute(pair, 'tensor', middle)  21.2 us
    ppermute x4, starting transfers between devices, planes_body(): across = lax.ppermute(pair, 'tensor', middle)  13.9 us
    ppermute x4, waiting for transfers between devices, planes_body(): onward = lax.ppermute(across, 'tensor', outward)  13.2 us
  transfers between devices with their start and end apart: 39, of which 15 were waited for; matrix products, arithmetic and copies ran while one was open for 26% of the time, Pallas kernels for 20%

commit v1 on v0

--- a/solution.py
+++ b/solution.py
@@ -55,6 +55,23 @@
 
 
 HBM = pltpu.MemorySpace.HBM
+
+
+def keep_body(source_ref, kept_ref, sem):
+    copy = pltpu.make_async_copy(source_ref, kept_ref, sem)
+    copy.start()
+    copy.wait()
+
+
+def keep_near(values):
+    return pl.pallas_call(
+        keep_body,
+        out_shape=pltpu.VMEM(values.shape, values.dtype),
+        in_specs=[pl.BlockSpec(memory_space=HBM)],
+        out_specs=pl.BlockSpec(memory_space=pltpu.VMEM),
+        scratch_shapes=[pltpu.SemaphoreType.DMA],
+        compiler_params=pltpu.CompilerParams(vmem_limit_bytes=16 * 2**20),
+    )(values)
 
 
 def weight_body(kinds, owners, tile, *refs):
@@ -168,18 +185,19 @@
 
 def grads_body(base_ref, direct_ref, got_ref, gate_ref, up_ref, *refs):
     gate_out, up_out = refs[-2:]
-    lane = 128
+    count = got_ref.shape[1]
+    lanes = 128 if count % 128 == 0 else count
 
     def one(j, carry):
-        at = (slice(None), pl.ds(pl.multiple_of(j * lane, lane), lane))
+        at = (slice(None), pl.ds(pl.multiple_of(j * lanes, lanes), lanes))
         folded = base_ref[at] + direct_ref[at].astype(jnp.float32) + got_ref[at].astype(jnp.float32)
         gate_out[at], up_out[at] = grads_of(folded, gate_ref[at], up_ref[at])
         return carry
 
-    lax.fori_loop(0, got_ref.shape[1] // lane, one, 0)
-
-
-def grads_into(base, direct, first, got, gate_turned, up_turned, column, before):
+    lax.fori_loop(0, count // lanes, one, 0)
+
+
+def grads_into(base, direct, got, gate_turned, up_turned, column, before):
     width, count = got.shape
     steps = 4 if width % 64 == 0 else 1
     tall = width // steps
@@ -188,7 +206,7 @@
         return pl.BlockSpec((tall, count), lambda i: (i, start // count))
 
     operands = [base, direct, got, gate_turned, up_turned]
-    specs = [at(first), at(first), at(0), at(column), at(column)]
+    specs = [at(0), at(0), at(0), at(column), at(column)]
     aliases = {}
     if before is not None:
         operands += before
@@ -222,7 +240,6 @@
     planes = lanes // 2
     quarter = rows // planes
     half = rows // 2
-    cut = half // 2
     me = lax.axis_index("fsdp")
     lane = lax.axis_index("tensor")
     plane = lane // 2
@@ -283,8 +300,10 @@
         token_scale = jnp.sum(onehots[k] * factor[None, :], axis=1)
         scaled[k] = (joined.astype(jnp.float32) * token_scale[:, None]).astype(jnp.bfloat16)
 
+    down_near = keep_near(down_weight)
+
     def back(k, lo, hi):
-        return masked_back(scaled[k][lo:hi], onehots[k][lo:hi], down_weight)
+        return masked_back(scaled[k][lo:hi], onehots[k][lo:hi], down_near)
 
     far1 = back(3, 0, half).astype(jnp.bfloat16)
     far2 = back(3, half, rows).astype(jnp.bfloat16)
@@ -293,14 +312,13 @@
     got2b = over(back(2, half, rows).astype(jnp.bfloat16), 2)
     near2 = (back(2, 0, half) + via1.astype(jnp.float32)).astype(jnp.bfloat16)
     near1 = (back(1, half, rows) + via2.astype(jnp.float32)).astype(jnp.bfloat16)
-    got2a = [over(near2[i * cut : (i + 1) * cut], 2) for i in range(2)]
-    got1b = [over(near1[i * cut : (i + 1) * cut], 1) for i in range(2)]
+    got2a, got1b = over(near2, 2), over(near1, 1)
     base_a = back(0, 0, half)
     base_b = back(0, half, rows)
 
     kinds_all = jnp.stack(kinds)[None, :, None, :]
     down_grad = None
-    for picked in ((0,), (1, 2)):
+    for picked in ((0, 1, 2),):
         labels = jnp.array(picked, jnp.int32)[:, None, None, None]
         marks = (kinds_all == labels).astype(jnp.float32)
         down_grad = weight_grad_of(
@@ -308,13 +326,8 @@
         )
 
     grads = None
-    for base, direct, first, got, column in (
-        (base_a, got1a, 0, got2a[0], 0),
-        (base_b, got2b, 0, got1b[0], half),
-        (base_a, got1a, cut, got2a[1], cut),
-        (base_b, got2b, cut, got1b[1], half + cut),
-    ):
-        grads = grads_into(base.T, direct.T, first, got.T, gate_turned, up_turned, column, grads)
+    for base, direct, got, column in ((base_a, got1a, got2a, 0), (base_b, got2b, got1b, half)):
+        grads = grads_into(base.T, direct.T, got.T, gate_turned, up_turned, column, grads)
     gate_grad, up_grad = grads
     return (down_grad, gate_grad.T, up_grad.T)
 

time: 302 us -> 302 us (level)
  the two profiles are of different devices: /device:TPU:8 before, /device:TPU:0 now
where the time goes in v1:
time: 302 us; the launch traced here: 298 us
  waiting for transfers between devices  131 us (43%)
  Pallas kernels  55.1 us (18%)
  starting transfers between devices  42.8 us (14%)
  matrix products  42.7 us (14%)
  other arithmetic  12.9 us (4%)
  local copies, waits for them, and re-layouts  12.2 us (4%)
    ppermute x18, waiting for transfers between devices, over(): return lax.ppermute(values, 'fsdp', [(i, i ^ step) for i in range(groups)])  70.3 us
    pallas_call x1, Pallas kernels, weight_grad_of(): pl.pallas_call(functools.partial(weight_body, kinds, tuple(owners), cols...  46.2 us
    dot_general x8, matrix products, masked_back(): lax.dot_general(masked, down_weight, (((0, 2), (0, 2)), ((), ())), prefer...  42.7 us
    ppermute x4, waiting for transfers between devices, planes_body(): onward = lax.ppermute(across, 'tensor', outward)  40.1 us
    ppermute x18, starting transfers between devices, over(): return lax.ppermute(values, 'fsdp', [(i, i ^ step) for i in range(groups)])  23.2 us
    ppermute x11, waiting for transfers between devices, along(): return lax.ppermute(values, 'tensor', [(i, i ^ step) for i in range(lanes)])  20.7 us
    ppermute x11, starting transfers between devices, along(): return lax.ppermute(values, 'tensor', [(i, i ^ step) for i in range(lanes)])  11.4 us
    unnamed x20, local copies, waits for them, and re-layouts  9.29 us
  transfers between devices with their start and end apart: 37, of which 16 were waited for; matrix products, arithmetic and copies ran while one was open for 20% of the time, Pallas kernels for 17%

profile of v1, /device:TPU:0, one launch (start us, length us, event | category | flops | bytes accessed | tf_op | source)
XLA Modules:
  0.0 298.1 jit_solution(6104912836989286565)
XLA Ops:
  0.6 4.0 %collective-permute-start.15 = (s32[1024]{0:T(1024)}, s32[1024]{0:T(1024)S(1)}, u32[]{:S(2)}, u32[]{:S(2)}) collective-permute-start(s32[1024]{0:T(1024)} %param.6), channel_id=1, source_target_pairs={{0,24},{8,16},{16,8},{24,0},{1,25},{9,17},{17,9},{25,1},{2,26},{10... | collective-permute-start | bytes 12296 | tf_op jit(solution)/shard_map/ppermute | solution.py:250
  5.3 3.5 %fusion.28 = (bf16[1376,512]{1,0:T(8,128)(2,1)S(1)}, bf16[1376,512]{1,0:T(8,128)(2,1)S(1)}) fusion(bf16[1376,1024]{1,0:T(8,128)(2,1)} %bitcast.86, bf16[1376,1024]{1,0:T(8,128)(2,1)} %bitcast.89), kind=kLoop, calls=%fused_computation.38 | loop fusion | flops 11272192 | bytes 8454144 | tf_op jit(solution)/shard_map/convert_element_type | solution.py:29
  10.8 2.1 constant_dynamic-slice_fusion
  12.8 3.6 %collective-permute-start.8 = (bf16[256,512]{1,0:T(8,128)(2,1)}, bf16[256,512]{1,0:T(8,128)(2,1)}, u32[]{:S(2)}, u32[]{:S(2)}) collective-permute-start(bf16[256,512]{1,0:T(8,128)(2,1)} %get-tuple-element.30), channel_id=1, source_target_pairs={{0,6},{1,7},{2,4},{3,5},{4,2},{5,3},{6,0},{7,1},{8,14},{9,15},{10,... | collective-permute-start | bytes 786440 | tf_op jit(solution)/shard_map/ppermute | solution.py:253
  16.6 3.4 %copy-done.2 = bf16[3,1376,1024]{2,1,0:T(8,128)(2,1)S(1)} copy-done((bf16[3,1376,1024]{2,1,0:T(8,128)(2,1)S(1)}, bf16[3,1376,1024]{2,1,0:T(8,128)(2,1)}, u32[]{:S(2)}) %copy-start.2) | copy-done | bytes 8454168
  20.7 3.4 %copy-done.3 = bf16[3,1376,1024]{2,1,0:T(8,128)(2,1)} copy-done((bf16[3,1376,1024]{2,1,0:T(8,128)(2,1)}, bf16[3,1376,1024]{2,1,0:T(8,128)(2,1)S(1)}, u32[]{:S(2)}) %copy-start.3) | copy-done | bytes 8454168
  25.1 12.7 %collective-permute-done.7 = bf16[256,512]{1,0:T(8,128)(2,1)S(1)} collective-permute-done((bf16[256,512]{1,0:T(8,128)(2,1)}, bf16[256,512]{1,0:T(8,128)(2,1)S(1)}, u32[]{:S(2)}, u32[]{:S(2)}) %collective-permute-start.7) | collective-permute-done | bytes 262176 | tf_op jit(solution)/shard_map/ppermute | solution.py:253
  42.7 5.5 %collective-permute-done.16 = bf16[256,512]{1,0:T(8,128)(2,1)S(1)} collective-permute-done((bf16[256,512]{1,0:T(8,128)(2,1)S(1)}, bf16[256,512]{1,0:T(8,128)(2,1)S(1)}, u32[]{:S(2)}, u32[]{:S(2)}) %collective-permute-start.16) | collective-permute-done | bytes 262176 | tf_op jit(solution)/shard_map/ppermute | solution.py:250
  51.5 4.2 %collective-permute-start.22 = (bf16[256,512]{1,0:T(8,128)(2,1)S(1)}, bf16[256,512]{1,0:T(8,128)(2,1)S(1)}, u32[]{:S(2)}, u32[]{:S(2)}) collective-permute-start(bf16[256,512]{1,0:T(8,128)(2,1)S(1)} %collective-permute-done.21), channel_id=1, source_target_pairs={{0,2},{1,3},{2,0},{3,1},{4,6},{5,7},{6,4},{7,5},{8,10},{9,11},{10,... | collective-permute-start | bytes 786440 | tf_op jit(solution)/shard_map/ppermute | solution.py:253
  58.1 4.7 %collective-permute-done.22 = bf16[256,512]{1,0:T(8,128)(2,1)S(1)} collective-permute-done((bf16[256,512]{1,0:T(8,128)(2,1)S(1)}, bf16[256,512]{1,0:T(8,128)(2,1)S(1)}, u32[]{:S(2)}, u32[]{:S(2)}) %collective-permute-start.22) | collective-permute-done | bytes 262176 | tf_op jit(solution)/shard_map/ppermute | solution.py:253
  63.8 2.1 collective-permute-done.27
  72.4 12.8 %collective-permute-done.11 = bf16[512,512]{1,0:T(8,128)(2,1)S(1)} collective-permute-done((bf16[512,512]{1,0:T(8,128)(2,1)S(1)}, bf16[512,512]{1,0:T(8,128)(2,1)S(1)}, u32[]{:S(2)}, u32[]{:S(2)}) %collective-permute-start.11) | collective-permute-done | bytes 524320 | tf_op jit(solution)/shard_map/ppermute | solution.py:291
  87.4 4.6 %collective-permute-done.19 = bf16[512,512]{1,0:T(8,128)(2,1)S(1)} collective-permute-done((bf16[512,512]{1,0:T(8,128)(2,1)S(1)}, bf16[512,512]{1,0:T(8,128)(2,1)S(1)}, u32[]{:S(2)}, u32[]{:S(2)}) %collective-permute-start.19) | collective-permute-done | bytes 524320 | tf_op jit(solution)/shard_map/ppermute | solution.py:291
  92.5 18.8 %collective-permute-done.24 = bf16[512,512]{1,0:T(8,128)(2,1)S(1)} collective-permute-done((bf16[512,512]{1,0:T(8,128)(2,1)S(1)}, bf16[512,512]{1,0:T(8,128)(2,1)S(1)}, u32[]{:S(2)}, u32[]{:S(2)}) %collective-permute-start.24) | collective-permute-done | bytes 524320 | tf_op jit(solution)/shard_map/ppermute | solution.py:291
  113.3 3.9 %collective-permute-done.29 = bf16[512,512]{1,0:T(8,128)(2,1)S(1)} collective-permute-done((bf16[512,512]{1,0:T(8,128)(2,1)S(1)}, bf16[512,512]{1,0:T(8,128)(2,1)S(1)}, u32[]{:S(2)}, u32[]{:S(2)}) %collective-permute-start.29) | collective-permute-done | bytes 524320 | tf_op jit(solution)/shard_map/ppermute | solution.py:291
  119.6 4.7 %convolution_bitcast_fusion.7.base_ref = f32[1376,512]{1,0:T(8,128)S(1)} fusion(bf16[3,1376,1024]{2,1,0:T(8,128)(2,1)S(1)} %bitcast.93, bf16[3,512]{1,0:T(4,128)(2,1)S(1)} %get-tuple-element.40, bf16[512,1024]{1,0:T(8,128)(2,1)S(1)} %get-tuple-element.24), kind=kOutput, calls=%fused_computation.15 | convolution fusion | flops 4330094592 | bytes 12323840 | tf_op jit(solution)/shard_map/dot_general | solution.py:43
  124.3 4.7 %convolution_bitcast_fusion.3.base_ref = f32[1376,512]{1,0:T(8,128)S(1)} fusion(bf16[3,1376,1024]{2,1,0:T(8,128)(2,1)S(1)} %bitcast.93, bf16[3,512]{1,0:T(4,128)(2,1)S(1)} %get-tuple-element.39, bf16[512,1024]{1,0:T(8,128)(2,1)S(1)} %get-tuple-element.23), kind=kOutput, calls=%fused_computation.11 | convolution fusion | flops 4330094592 | bytes 12323840 | tf_op jit(solution)/shard_map/dot_general | solution.py:43
  130.8 4.8 %fusion.11 = bf16[512,1376]{0,1:T(8,128)(2,1)S(1)} fusion(bf16[3,1376,1024]{2,1,0:T(8,128)(2,1)S(1)} %bitcast.93, bf16[3,512]{1,0:T(4,128)(2,1)S(1)} %get-tuple-element.36, bf16[512,1024]{1,0:T(8,128)(2,1)S(1)} %get-tuple-element.20), kind=kOutput, calls=%fused_computation.25 | convolution fusion | flops 4330799104 | bytes 10914816 | tf_op jit(solution)/shard_map/dot_general | solution.py:43
  139.7 6.0 %fusion.17 = bf16[512,1376]{0,1:T(8,128)(2,1)} fusion(bf16[3,1376,1024]{2,1,0:T(8,128)(2,1)S(1)} %bitcast.93, bf16[3,512]{1,0:T(4,128)(2,1)S(1)} %get-tuple-element.35, bf16[512,1024]{1,0:T(8,128)(2,1)S(1)} %get-tuple-element.19), kind=kOutput, calls=%fused_computation.27 | convolution fusion | flops 4330799104 | bytes 10914816 | tf_op jit(solution)/shard_map/dot_general | solution.py:43
  147.2 4.8 %fusion.8 = bf16[512,1376]{0,1:T(8,128)(2,1)S(1)} fusion(bf16[3,1376,1024]{2,1,0:T(8,128)(2,1)S(1)} %bitcast.93, bf16[3,512]{1,0:T(4,128)(2,1)S(1)} %get-tuple-element.34, bf16[512,1024]{1,0:T(8,128)(2,1)S(1)} %get-tuple-element.18), kind=kOutput, calls=%fused_computation.24 | convolution fusion | flops 4330799104 | bytes 10914816 | tf_op jit(solution)/shard_map/dot_general | solution.py:43
  152.0 4.8 %fusion.14 = bf16[512,1376]{0,1:T(8,128)(2,1)S(1)} fusion(bf16[3,1376,1024]{2,1,0:T(8,128)(2,1)S(1)} %bitcast.93, bf16[3,512]{1,0:T(4,128)(2,1)S(1)} %get-tuple-element.37, bf16[512,1024]{1,0:T(8,128)(2,1)S(1)} %get-tuple-element.21), kind=kOutput, calls=%fused_computation.26 | convolution fusion | flops 4330799104 | bytes 10914816 | tf_op jit(solution)/shard_map/dot_general | solution.py:43
  157.9 11.6 %collective-permute-done.32 = bf16[512,1376]{0,1:T(8,128)(2,1)} collective-permute-done((bf16[512,1376]{0,1:T(8,128)(2,1)S(1)}, bf16[512,1376]{0,1:T(8,128)(2,1)}, u32[]{:S(2)}, u32[]{:S(2)}) %collective-permute-start.32) | collective-permute-done | bytes 1409056 | tf_op jit(solution)/shard_map/ppermute | solution.py:250
  171.0 6.1 %add_convert_fusion.1 = bf16[512,1376]{0,1:T(8,128)(2,1)S(1)} fusion(bf16[512,1376]{0,1:T(8,128)(2,1)} %collective-permute-done.32, bf16[3,1376,1024]{2,1,0:T(8,128)(2,1)S(1)} %bitcast.93, bf16[3,512]{1,0:T(4,128)(2,1)S(1)} %get-tuple-element.38, bf16[512,1024]{1,0:T(8,128)(2,1)S(1)} %get-tuple-element.22), kind=kOutput, calls=%fused_computation.37 | convolution fusion | flops 4332208128 | bytes 12323840 | tf_op jit(solution)/shard_map/dot_general | solution.py:43
  177.1 2.7 collective-permute-done.35
  180.3 6.9 %add_convert_fusion = bf16[512,1376]{0,1:T(8,128)(2,1)} fusion(bf16[512,1376]{0,1:T(8,128)(2,1)} %collective-permute-done.35, bf16[3,1376,1024]{2,1,0:T(8,128)(2,1)S(1)} %bitcast.93, bf16[3,512]{1,0:T(4,128)(2,1)S(1)} %get-tuple-element.33, bf16[512,1024]{1,0:T(8,128)(2,1)S(1)} %get-tuple-element.17), kind=kOutput, calls=%fused_computation.36 | convolution fusion | flops 4332208128 | bytes 12323840 | tf_op jit(solution)/shard_map/dot_general | solution.py:43
  188.8 10.8 %collective-permute-done.3.refs_5_ = bf16[1376,512]{1,0:T(8,128)(2,1)S(1)} collective-permute-done((bf16[1376,512]{1,0:T(8,128)(2,1)S(1)}, bf16[1376,512]{1,0:T(8,128)(2,1)S(1)}, u32[]{:S(2)}, u32[]{:S(2)}) %collective-permute-start.3) | collective-permute-done | bytes 1409056 | tf_op jit(solution)/shard_map/ppermute | solution.py:250
  202.2 7.8 %collective-permute-done.4.refs_6_ = bf16[1376,512]{1,0:T(8,128)(2,1)} collective-permute-done((bf16[1376,512]{1,0:T(8,128)(2,1)}, bf16[1376,512]{1,0:T(8,128)(2,1)}, u32[]{:S(2)}, u32[]{:S(2)}) %collective-permute-start.4) | collective-permute-done | bytes 1409056 | tf_op jit(solution)/shard_map/ppermute | solution.py:250
  210.5 19.4 %collective-permute-done.5.refs_7_ = bf16[1376,512]{1,0:T(8,128)(2,1)} collective-permute-done((bf16[1376,512]{1,0:T(8,128)(2,1)}, bf16[1376,512]{1,0:T(8,128)(2,1)}, u32[]{:S(2)}, u32[]{:S(2)}) %collective-permute-start.5) | collective-permute-done | bytes 1409056 | tf_op jit(solution)/shard_map/ppermute | solution.py:250
  231.3 46.2 %shard_map.85 = f32[3,1376,1024]{2,1,0:T(8,128)} custom-call(bf16[1376,512]{1,0:T(8,128)(2,1)S(1)} %get-tuple-element.16.refs_0_, bf16[1376,512]{1,0:T(8,128)(2,1)S(1)} %get-tuple-element.15.refs_1_, bf16[1376,512]{1,0:T(8,128)(2,1)} %collective-permute-done.refs_2_, bf16[1376,512]{1,0:T(8,128)(2,1)} %collective-permute-done.1.refs_3_, ...), custom_call_target="tpu_custom_call" | custom-call | flops 34628173824 | bytes 36569088 | tf_op jit(solution)/shard_map/pallas_call | solution.py:163
  277.5 12.2 %collective-permute-done.36 = bf16[512,1376]{0,1:T(8,128)(2,1)S(1)} collective-permute-done((bf16[512,1376]{0,1:T(8,128)(2,1)}, bf16[512,1376]{0,1:T(8,128)(2,1)S(1)}, u32[]{:S(2)}, u32[]{:S(2)}) %collective-permute-start.36) | collective-permute-done | bytes 1409056 | tf_op jit(solution)/shard_map/ppermute | solution.py:250
  289.7 3.5 %shard_map.87 = (bf16[1376,1024]{1,0:T(8,128)(2,1)}, bf16[1376,1024]{1,0:T(8,128)(2,1)}) custom-call(f32[1376,512]{1,0:T(8,128)S(1)} %convolution_bitcast_fusion.3.base_ref, bf16[1376,512]{1,0:T(8,128)(2,1)S(1)} %bitcast.95, bf16[1376,512]{1,0:T(8,128)(2,1)S(1)} %bitcast.96, bf16[1376,1024]{1,0:T(8,128)(2,1)S(1)} %bitcast.90, bf16[1376,1024]{1,0:T(8,128)(2,1)S(1)} %bitcast.87), custom_call_target="tpu_custom_call" | custom-call | flops 14090240 | bytes 11272192 | tf_op jit(solution)/shard_map/pallas_call | solution.py:216
  293.2 4.7 %shard_map.88 = (bf16[1376,1024]{1,0:T(8,128)(2,1)}, bf16[1376,1024]{1,0:T(8,128)(2,1)}) custom-call(f32[1376,512]{1,0:T(8,128)S(1)} %convolution_bitcast_fusion.7.base_ref, bf16[1376,512]{1,0:T(8,128)(2,1)} %bitcast.22.direct_ref, bf16[1376,512]{1,0:T(8,128)(2,1)S(1)} %bitcast.94, ...), custom_call_target="tpu_custom_call", output_to_operand_aliasing={{0}: (5, {}), {1}: (6, {})} | custom-call | flops 14090240 | bytes 11272192 | tf_op jit(solution)/shard_map/pallas_call | solution.py:216
  (115 shorter events, 45.8 us)
Async XLA Ops:
  0.6 23.5 %collective-permute-start.15 = (s32[1024]{0:T(1024)}, s32[1024]{0:T(1024)S(1)}, u32[]{:S(2)}, u32[]{:S(2)}) collective-permute-start(s32[1024]{0:T(1024)} %param.6), channel_id=1, source_target_pairs={{0,24},{8,16},{16,8},{24,0},{1,25},{9,17},{17,9},{25,1},{2,26},{10... | collective-permute-start | bytes 12296 | tf_op jit(solution)/shard_map/ppermute | solution.py:250
  4.6 19.5 %collective-permute-start.14 = (s32[1024]{0:T(1024)}, s32[1024]{0:T(1024)S(1)}, u32[]{:S(2)}, u32[]{:S(2)}) collective-permute-start(s32[1024]{0:T(1024)} %param.6), channel_id=1, source_target_pairs={{0,16},{8,24},{16,0},{24,8},{1,17},{9,25},{17,1},{25,9},{2,18},{10... | collective-permute-start | bytes 12296 | tf_op jit(solution)/shard_map/ppermute | solution.py:250
  5.1 19.9 %collective-permute-start.13 = (s32[1024]{0:T(1024)}, s32[1024]{0:T(1024)S(1)}, u32[]{:S(2)}, u32[]{:S(2)}) collective-permute-start(s32[1024]{0:T(1024)} %param.6), channel_id=1, source_target_pairs={{0,8},{8,0},{16,24},{24,16},{1,9},{9,1},{17,25},{25,17},{2,10},{10... | collective-permute-start | bytes 12296 | tf_op jit(solution)/shard_map/ppermute | solution.py:250
  8.8 178.4 %collective-permute-start = (bf16[1376,512]{1,0:T(8,128)(2,1)S(1)}, bf16[1376,512]{1,0:T(8,128)(2,1)}, u32[]{:S(2)}, u32[]{:S(2)}) collective-permute-start(bf16[1376,512]{1,0:T(8,128)(2,1)S(1)} %get-tuple-element.16.refs_0_), channel_id=1, source_target_pairs={{0,8},{8,0},{16,24},{24,16},{1,9},{9,1},{17,25},{25,17},{2,10},{10... | collective-permute-start | bytes 4227080 | tf_op jit(solution)/shard_map/ppermute | solution.py:250
  12.8 12.3 %collective-permute-start.8 = (bf16[256,512]{1,0:T(8,128)(2,1)}, bf16[256,512]{1,0:T(8,128)(2,1)}, u32[]{:S(2)}, u32[]{:S(2)}) collective-permute-start(bf16[256,512]{1,0:T(8,128)(2,1)} %get-tuple-element.30), channel_id=1, source_target_pairs={{0,6},{1,7},{2,4},{3,5},{4,2},{5,3},{6,0},{7,1},{8,14},{9,15},{10,... | collective-permute-start | bytes 786440 | tf_op jit(solution)/shard_map/ppermute | solution.py:253
  24.1 13.7 %collective-permute-start.7 = (bf16[256,512]{1,0:T(8,128)(2,1)}, bf16[256,512]{1,0:T(8,128)(2,1)S(1)}, u32[]{:S(2)}, u32[]{:S(2)}) collective-permute-start(bf16[256,512]{1,0:T(8,128)(2,1)} %get-tuple-element.31), channel_id=1, source_target_pairs={{0,4},{1,5},{2,6},{3,7},{4,0},{5,1},{6,2},{7,3},{8,12},{9,13},{10,... | collective-permute-start | bytes 786440 | tf_op jit(solution)/shard_map/ppermute | solution.py:253
  24.2 13.6 %collective-permute-start.6 = (bf16[256,512]{1,0:T(8,128)(2,1)S(1)}, bf16[256,512]{1,0:T(8,128)(2,1)S(1)}, u32[]{:S(2)}, u32[]{:S(2)}) collective-permute-start(bf16[256,512]{1,0:T(8,128)(2,1)S(1)} %get-tuple-element.32), channel_id=1, source_target_pairs={{0,2},{1,3},{2,0},{3,1},{4,6},{5,7},{6,4},{7,5},{8,10},{9,11},{10,... | collective-permute-start | bytes 786440 | tf_op jit(solution)/shard_map/ppermute | solution.py:253
  39.6 10.7 %collective-permute-start.9 = (bf16[256,512]{1,0:T(8,128)(2,1)S(1)}, bf16[256,512]{1,0:T(8,128)(2,1)S(1)}, u32[]{:S(2)}, u32[]{:S(2)}) collective-permute-start(bf16[256,512]{1,0:T(8,128)(2,1)S(1)} %get-tuple-element.28), channel_id=1, source_target_pairs={{0,2},{1,3},{2,0},{3,1},{4,6},{5,7},{6,4},{7,5},{8,10},{9,11},{10,... | collective-permute-start | bytes 786440 | tf_op jit(solution)/shard_map/ppermute | solution.py:253
  39.6 11.9 %collective-permute-start.21 = (bf16[256,512]{1,0:T(8,128)(2,1)S(1)}, bf16[256,512]{1,0:T(8,128)(2,1)S(1)}, u32[]{:S(2)}, u32[]{:S(2)}) collective-permute-start(bf16[256,512]{1,0:T(8,128)(2,1)S(1)} %get-tuple-element.26), channel_id=1, source_target_pairs={{0,16},{8,24},{16,0},{24,8},{1,17},{9,25},{17,1},{25,9},{2,18},{10... | collective-permute-start | bytes 786440 | tf_op jit(solution)/shard_map/ppermute | solution.py:250
  41.2 14.6 %collective-permute-start.26 = (bf16[256,512]{1,0:T(8,128)(2,1)S(1)}, bf16[256,512]{1,0:T(8,128)(2,1)S(1)}, u32[]{:S(2)}, u32[]{:S(2)}) collective-permute-start(bf16[256,512]{1,0:T(8,128)(2,1)S(1)} %get-tuple-element.25), channel_id=1, source_target_pairs={{0,24},{8,16},{16,8},{24,0},{1,25},{9,17},{17,9},{25,1},{2,26},{10... | collective-permute-start | bytes 786440 | tf_op jit(solution)/shard_map/ppermute | solution.py:250
  50.6 16.2 %collective-permute-start.10 = (bf16[512,512]{1,0:T(8,128)(2,1)S(1)}, bf16[512,512]{1,0:T(8,128)(2,1)S(1)}, u32[]{:S(2)}, u32[]{:S(2)}) collective-permute-start(bf16[512,512]{1,0:T(8,128)(2,1)S(1)} %maximum_select_fusion.8), channel_id=1, source_target_pairs={{2,4},{3,5},{4,2},{5,3},{10,12},{11,13},{12,10},{13,11},{18,20},{1... | collective-permute-start | bytes 1572872 | tf_op jit(solution)/shard_map/ppermute | solution.py:290
  51.5 11.4 %collective-permute-start.22 = (bf16[256,512]{1,0:T(8,128)(2,1)S(1)}, bf16[256,512]{1,0:T(8,128)(2,1)S(1)}, u32[]{:S(2)}, u32[]{:S(2)}) collective-permute-start(bf16[256,512]{1,0:T(8,128)(2,1)S(1)} %collective-permute-done.21), channel_id=1, source_target_pairs={{0,2},{1,3},{2,0},{3,1},{4,6},{5,7},{6,4},{7,5},{8,10},{9,11},{10,... | collective-permute-start | bytes 786440 | tf_op jit(solution)/shard_map/ppermute | solution.py:253
  55.8 10.0 %collective-permute-start.27 = (bf16[256,512]{1,0:T(8,128)(2,1)S(1)}, bf16[256,512]{1,0:T(8,128)(2,1)S(1)}, u32[]{:S(2)}, u32[]{:S(2)}) collective-permute-start(bf16[256,512]{1,0:T(8,128)(2,1)S(1)} %collective-permute-done.26), channel_id=1, source_target_pairs={{0,2},{1,3},{2,0},{3,1},{4,6},{5,7},{6,4},{7,5},{8,10},{9,11},{10,... | collective-permute-start | bytes 786440 | tf_op jit(solution)/shard_map/ppermute | solution.py:253
  57.3 10.8 %collective-permute-start.18 = (bf16[512,512]{1,0:T(8,128)(2,1)S(1)}, bf16[512,512]{1,0:T(8,128)(2,1)S(1)}, u32[]{:S(2)}, u32[]{:S(2)}) collective-permute-start(bf16[512,512]{1,0:T(8,128)(2,1)S(1)} %maximum_select_fusion.9), channel_id=1, source_target_pairs={{2,4},{3,5},{4,2},{5,3},{10,12},{11,13},{12,10},{13,11},{18,20},{1... | collective-permute-start | bytes 1572872 | tf_op jit(solution)/shard_map/ppermute | solution.py:290
  66.8 18.5 %collective-permute-start.11 = (bf16[512,512]{1,0:T(8,128)(2,1)S(1)}, bf16[512,512]{1,0:T(8,128)(2,1)S(1)}, u32[]{:S(2)}, u32[]{:S(2)}) collective-permute-start(bf16[512,512]{1,0:T(8,128)(2,1)S(1)} %collective-permute-done.10), channel_id=1, source_target_pairs={{2,0},{3,1},{4,6},{5,7},{10,8},{11,9},{12,14},{13,15},{18,16},{19,... | collective-permute-start | bytes 1572872 | tf_op jit(solution)/shard_map/ppermute | solution.py:291
  68.1 23.9 %collective-permute-start.19 = (bf16[512,512]{1,0:T(8,128)(2,1)S(1)}, bf16[512,512]{1,0:T(8,128)(2,1)S(1)}, u32[]{:S(2)}, u32[]{:S(2)}) collective-permute-start(bf16[512,512]{1,0:T(8,128)(2,1)S(1)} %collective-permute-done.18), channel_id=1, source_target_pairs={{2,0},{3,1},{4,6},{5,7},{10,8},{11,9},{12,14},{13,15},{18,16},{19,... | collective-permute-start | bytes 1572872 | tf_op jit(solution)/shard_map/ppermute | solution.py:291
  69.6 87.8 %collective-permute-start.2 = (bf16[1376,512]{1,0:T(8,128)(2,1)S(1)}, bf16[1376,512]{1,0:T(8,128)(2,1)}, u32[]{:S(2)}, u32[]{:S(2)}) collective-permute-start(bf16[1376,512]{1,0:T(8,128)(2,1)S(1)} %get-tuple-element.16.refs_0_), channel_id=1, source_target_pairs={{0,16},{8,24},{16,0},{24,8},{1,17},{9,25},{17,1},{25,9},{2,18},{10... | collective-permute-start | bytes 4227080 | tf_op jit(solution)/shard_map/ppermute | solution.py:250
  71.1 40.2 %collective-permute-start.24 = (bf16[512,512]{1,0:T(8,128)(2,1)S(1)}, bf16[512,512]{1,0:T(8,128)(2,1)S(1)}, u32[]{:S(2)}, u32[]{:S(2)}) collective-permute-start(bf16[512,512]{1,0:T(8,128)(2,1)S(1)} %collective-permute-done.23), channel_id=1, source_target_pairs={{2,0},{3,1},{4,6},{5,7},{10,8},{11,9},{12,14},{13,15},{18,16},{19,... | collective-permute-start | bytes 1572872 | tf_op jit(solution)/shard_map/ppermute | solution.py:291
  85.3 31.9 %collective-permute-start.29 = (bf16[512,512]{1,0:T(8,128)(2,1)S(1)}, bf16[512,512]{1,0:T(8,128)(2,1)S(1)}, u32[]{:S(2)}, u32[]{:S(2)}) collective-permute-start(bf16[512,512]{1,0:T(8,128)(2,1)S(1)} %collective-permute-done.28), channel_id=1, source_target_pairs={{2,0},{3,1},{4,6},{5,7},{10,8},{11,9},{12,14},{13,15},{18,16},{19,... | collective-permute-start | bytes 1572872 | tf_op jit(solution)/shard_map/ppermute | solution.py:291
  92.0 25.7 %collective-permute-start.12 = (bf16[1024,512]{1,0:T(8,128)(2,1)S(1)}, bf16[1024,512]{1,0:T(8,128)(2,1)S(1)}, u32[]{:S(2)}, u32[]{:S(2)}) collective-permute-start(bf16[1024,512]{1,0:T(8,128)(2,1)S(1)} %maximum_select_fusion.4), channel_id=1, source_target_pairs={{0,1},{1,0},{2,3},{3,2},{4,5},{5,4},{6,7},{7,6},{8,9},{9,8},{10,11... | collective-permute-start | bytes 3145736 | tf_op jit(solution)/shard_map/ppermute | solution.py:253
  111.3 45.4 %collective-permute-start.1 = (bf16[1376,512]{1,0:T(8,128)(2,1)S(1)}, bf16[1376,512]{1,0:T(8,128)(2,1)}, u32[]{:S(2)}, u32[]{:S(2)}) collective-permute-start(bf16[1376,512]{1,0:T(8,128)(2,1)S(1)} %get-tuple-element.15.refs_1_), channel_id=1, source_target_pairs={{0,8},{8,0},{16,24},{24,16},{1,9},{9,1},{17,25},{25,17},{2,10},{10... | collective-permute-start | bytes 4227080 | tf_op jit(solution)/shard_map/ppermute | solution.py:250
  117.2 21.2 %collective-permute-start.20 = (bf16[1024,512]{1,0:T(8,128)(2,1)S(1)}, bf16[1024,512]{1,0:T(8,128)(2,1)S(1)}, u32[]{:S(2)}, u32[]{:S(2)}) collective-permute-start(bf16[1024,512]{1,0:T(8,128)(2,1)S(1)} %maximum_select_fusion.5), channel_id=1, source_target_pairs={{0,1},{1,0},{2,3},{3,2},{4,5},{5,4},{6,7},{7,6},{8,9},{9,8},{10,11... | collective-permute-start | bytes 3145736 | tf_op jit(solution)/shard_map/ppermute | solution.py:253
  117.7 11.2 %collective-permute-start.30 = (bf16[1024,512]{1,0:T(8,128)(2,1)S(1)}, bf16[1024,512]{1,0:T(8,128)(2,1)S(1)}, u32[]{:S(2)}, u32[]{:S(2)}) collective-permute-start(bf16[1024,512]{1,0:T(8,128)(2,1)S(1)} %maximum_select_fusion.7), channel_id=1, source_target_pairs={{0,1},{1,0},{2,3},{3,2},{4,5},{5,4},{6,7},{7,6},{8,9},{9,8},{10,11... | collective-permute-start | bytes 3145736 | tf_op jit(solution)/shard_map/ppermute | solution.py:253
  135.6 33.9 %collective-permute-start.32 = (bf16[512,1376]{0,1:T(8,128)(2,1)S(1)}, bf16[512,1376]{0,1:T(8,128)(2,1)}, u32[]{:S(2)}, u32[]{:S(2)}) collective-permute-start(bf16[512,1376]{0,1:T(8,128)(2,1)S(1)} %fusion.11), channel_id=1, source_target_pairs={{0,16},{8,24},{16,0},{24,8},{1,17},{9,25},{17,1},{25,9},{2,18},{10... | collective-permute-start | bytes 4227080 | tf_op jit(solution)/shard_map/ppermute | solution.py:250
  145.6 34.1 %collective-permute-start.35 = (bf16[512,1376]{0,1:T(8,128)(2,1)}, bf16[512,1376]{0,1:T(8,128)(2,1)}, u32[]{:S(2)}, u32[]{:S(2)}) collective-permute-start(bf16[512,1376]{0,1:T(8,128)(2,1)} %fusion.17), channel_id=1, source_target_pairs={{0,8},{8,0},{16,24},{24,16},{1,9},{9,1},{17,25},{25,17},{2,10},{10... | collective-permute-start | bytes 4227080 | tf_op jit(solution)/shard_map/ppermute | solution.py:250
  156.8 42.9 %collective-permute-start.3 = (bf16[1376,512]{1,0:T(8,128)(2,1)S(1)}, bf16[1376,512]{1,0:T(8,128)(2,1)S(1)}, u32[]{:S(2)}, u32[]{:S(2)}) collective-permute-start(bf16[1376,512]{1,0:T(8,128)(2,1)S(1)} %get-tuple-element.15.refs_1_), channel_id=1, source_target_pairs={{0,16},{8,24},{16,0},{24,8},{1,17},{9,25},{17,1},{25,9},{2,18},{10... | collective-permute-start | bytes 4227080 | tf_op jit(solution)/shard_map/ppermute | solution.py:250
  157.4 52.6 %collective-permute-start.4 = (bf16[1376,512]{1,0:T(8,128)(2,1)}, bf16[1376,512]{1,0:T(8,128)(2,1)}, u32[]{:S(2)}, u32[]{:S(2)}) collective-permute-start(bf16[1376,512]{1,0:T(8,128)(2,1)} %collective-permute-done.2.refs_4_), channel_id=1, source_target_pairs={{0,8},{8,0},{16,24},{24,16},{1,9},{9,1},{17,25},{25,17},{2,10},{10... | collective-permute-start | bytes 4227080 | tf_op jit(solution)/shard_map/ppermute | solution.py:250
  169.5 60.4 %collective-permute-start.5 = (bf16[1376,512]{1,0:T(8,128)(2,1)}, bf16[1376,512]{1,0:T(8,128)(2,1)}, u32[]{:S(2)}, u32[]{:S(2)}) collective-permute-start(bf16[1376,512]{1,0:T(8,128)(2,1)} %collective-permute-done.1.refs_3_), channel_id=1, source_target_pairs={{0,16},{8,24},{16,0},{24,8},{1,17},{9,25},{17,1},{25,9},{2,18},{10... | collective-permute-start | bytes 4227080 | tf_op jit(solution)/shard_map/ppermute | solution.py:250
  179.8 113.5 %collective-permute-start.31 = (bf16[512,1376]{0,1:T(8,128)(2,1)S(1)}, bf16[512,1376]{0,1:T(8,128)(2,1)}, u32[]{:S(2)}, u32[]{:S(2)}) collective-permute-start(bf16[512,1376]{0,1:T(8,128)(2,1)S(1)} %fusion.8), channel_id=1, source_target_pairs={{0,16},{8,24},{16,0},{24,8},{1,17},{9,25},{17,1},{25,9},{2,18},{10... | collective-permute-start | bytes 4227080 | tf_op jit(solution)/shard_map/ppermute | solution.py:250
  187.2 90.3 %collective-permute-start.34 = (bf16[512,1376]{0,1:T(8,128)(2,1)S(1)}, bf16[512,1376]{0,1:T(8,128)(2,1)S(1)}, u32[]{:S(2)}, u32[]{:S(2)}) collective-permute-start(bf16[512,1376]{0,1:T(8,128)(2,1)S(1)} %fusion.14), channel_id=1, source_target_pairs={{0,8},{8,0},{16,24},{24,16},{1,9},{9,1},{17,25},{25,17},{2,10},{10... | collective-permute-start | bytes 4227080 | tf_op jit(solution)/shard_map/ppermute | solution.py:250
  200.7 92.5 %collective-permute-start.33 = (bf16[512,1376]{0,1:T(8,128)(2,1)S(1)}, bf16[512,1376]{0,1:T(8,128)(2,1)S(1)}, u32[]{:S(2)}, u32[]{:S(2)}) collective-permute-start(bf16[512,1376]{0,1:T(8,128)(2,1)S(1)} %add_convert_fusion.1), channel_id=1, source_target_pairs={{0,8},{8,0},{16,24},{24,16},{1,9},{9,1},{17,25},{25,17},{2,10},{10... | collective-permute-start | bytes 4227080 | tf_op jit(solution)/shard_map/ppermute | solution.py:250
  210.0 79.7 %collective-permute-start.36 = (bf16[512,1376]{0,1:T(8,128)(2,1)}, bf16[512,1376]{0,1:T(8,128)(2,1)S(1)}, u32[]{:S(2)}, u32[]{:S(2)}) collective-permute-start(bf16[512,1376]{0,1:T(8,128)(2,1)} %add_convert_fusion), channel_id=1, source_target_pairs={{0,16},{8,24},{16,0},{24,8},{1,17},{9,25},{17,1},{25,9},{2,18},{10... | collective-permute-start | bytes 4227080 | tf_op jit(solution)/shard_map/ppermute | solution.py:250
  (15 other events, 303.7 us)

commit v2 on v1

--- a/solution.py
+++ b/solution.py
@@ -20,7 +20,7 @@
 def activations(gate_pre, up_pre):
     gate_val = gate_pre.astype(jnp.float32)
     up_val = up_pre.astype(jnp.float32)
-    sigmoid_g = jax.nn.sigmoid(gate_val)
+    sigmoid_g = 0.5 * jnp.tanh(0.5 * gate_val) + 0.5
     return gate_val, up_val, sigmoid_g, gate_val * sigmoid_g
 
 
@@ -30,9 +30,9 @@
 
 
 def grads_of(folded, gate_pre, up_pre):
-    gate_val, up_val, sigmoid_g, active = activations(gate_pre, up_pre)
+    _, up_val, sigmoid_g, active = activations(gate_pre, up_pre)
     up_grad = (folded * active).astype(jnp.bfloat16)
-    slope = sigmoid_g * (1.0 + gate_val * (1.0 - sigmoid_g))
+    slope = sigmoid_g + active * (1.0 - sigmoid_g)
     gate_grad = (folded * up_val * slope).astype(jnp.bfloat16)
     return gate_grad, up_grad
 

time: 302 us -> 303 us (level)
  no operation moved by 1% of the time
where the time goes in v2:
time: 303 us; the launch traced here: 298 us
  waiting for transfers between devices  131 us (43%)
  Pallas kernels  55.2 us (18%)
  starting transfers between devices  42.8 us (14%)
  matrix products  42.7 us (14%)
  other arithmetic  12.9 us (4%)
  local copies, waits for them, and re-layouts  12.2 us (4%)
    ppermute x18, waiting for transfers between devices, over(): return lax.ppermute(values, 'fsdp', [(i, i ^ step) for i in range(groups)])  70.3 us
    pallas_call x1, Pallas kernels, weight_grad_of(): pl.pallas_call(functools.partial(weight_body, kinds, tuple(owners), cols...  46.2 us
    dot_general x8, matrix products, masked_back(): lax.dot_general(masked, down_weight, (((0, 2), (0, 2)), ((), ())), prefer...  42.7 us
    ppermute x4, waiting for transfers between devices, planes_body(): onward = lax.ppermute(across, 'tensor', outward)  40.1 us
    ppermute x18, starting transfers between devices, over(): return lax.ppermute(values, 'fsdp', [(i, i ^ step) for i in range(groups)])  23.2 us
    ppermute x11, waiting for transfers between devices, along(): return lax.ppermute(values, 'tensor', [(i, i ^ step) for i in range(lanes)])  20.7 us
    ppermute x11, starting transfers between devices, along(): return lax.ppermute(values, 'tensor', [(i, i ^ step) for i in range(lanes)])  11.4 us
    unnamed x20, local copies, waits for them, and re-layouts  9.29 us
  transfers between devices with their start and end apart: 37, of which 16 were waited for; matrix products, arithmetic and copies ran while one was open for 20% of the time, Pallas kernels for 17%

profile of v2, /device:TPU:0, one launch (start us, length us, event | category | flops | bytes accessed | tf_op | source)
XLA Modules:
  0.0 298.3 jit_solution(12629376453283226776)
XLA Ops:
  0.6 4.0 %collective-permute-start.15 = (s32[1024]{0:T(1024)}, s32[1024]{0:T(1024)S(1)}, u32[]{:S(2)}, u32[]{:S(2)}) collective-permute-start(s32[1024]{0:T(1024)} %param.6), channel_id=1, source_target_pairs={{0,24},{8,16},{16,8},{24,0},{1,25},{9,17},{17,9},{25,1},{2,26},{10... | collective-permute-start | bytes 12296 | tf_op jit(solution)/shard_map/ppermute | solution.py:250
  5.3 3.5 %fusion.29 = (bf16[1376,512]{1,0:T(8,128)(2,1)S(1)}, bf16[1376,512]{1,0:T(8,128)(2,1)S(1)}) fusion(bf16[1376,1024]{1,0:T(8,128)(2,1)} %bitcast.86, bf16[1376,1024]{1,0:T(8,128)(2,1)} %bitcast.89), kind=kLoop, calls=%fused_computation.37 | loop fusion | flops 11272192 | bytes 8454144 | tf_op jit(solution)/shard_map/convert_element_type | solution.py:29
  10.8 2.1 constant_dynamic-slice_fusion
  12.8 3.6 %collective-permute-start.8 = (bf16[256,512]{1,0:T(8,128)(2,1)}, bf16[256,512]{1,0:T(8,128)(2,1)}, u32[]{:S(2)}, u32[]{:S(2)}) collective-permute-start(bf16[256,512]{1,0:T(8,128)(2,1)} %get-tuple-element.30), channel_id=1, source_target_pairs={{0,6},{1,7},{2,4},{3,5},{4,2},{5,3},{6,0},{7,1},{8,14},{9,15},{10,... | collective-permute-start | bytes 786440 | tf_op jit(solution)/shard_map/ppermute | solution.py:253
  16.7 3.4 %copy-done.2 = bf16[3,1376,1024]{2,1,0:T(8,128)(2,1)S(1)} copy-done((bf16[3,1376,1024]{2,1,0:T(8,128)(2,1)S(1)}, bf16[3,1376,1024]{2,1,0:T(8,128)(2,1)}, u32[]{:S(2)}) %copy-start.2) | copy-done | bytes 8454168
  20.7 3.4 %copy-done.3 = bf16[3,1376,1024]{2,1,0:T(8,128)(2,1)} copy-done((bf16[3,1376,1024]{2,1,0:T(8,128)(2,1)}, bf16[3,1376,1024]{2,1,0:T(8,128)(2,1)S(1)}, u32[]{:S(2)}) %copy-start.3) | copy-done | bytes 8454168
  25.1 12.7 %collective-permute-done.7 = bf16[256,512]{1,0:T(8,128)(2,1)S(1)} collective-permute-done((bf16[256,512]{1,0:T(8,128)(2,1)}, bf16[256,512]{1,0:T(8,128)(2,1)S(1)}, u32[]{:S(2)}, u32[]{:S(2)}) %collective-permute-start.7) | collective-permute-done | bytes 262176 | tf_op jit(solution)/shard_map/ppermute | solution.py:253
  42.7 5.5 %collective-permute-done.16 = bf16[256,512]{1,0:T(8,128)(2,1)S(1)} collective-permute-done((bf16[256,512]{1,0:T(8,128)(2,1)S(1)}, bf16[256,512]{1,0:T(8,128)(2,1)S(1)}, u32[]{:S(2)}, u32[]{:S(2)}) %collective-permute-start.16) | collective-permute-done | bytes 262176 | tf_op jit(solution)/shard_map/ppermute | solution.py:250
  51.5 4.2 %collective-permute-start.22 = (bf16[256,512]{1,0:T(8,128)(2,1)S(1)}, bf16[256,512]{1,0:T(8,128)(2,1)S(1)}, u32[]{:S(2)}, u32[]{:S(2)}) collective-permute-start(bf16[256,512]{1,0:T(8,128)(2,1)S(1)} %collective-permute-done.21), channel_id=1, source_target_pairs={{0,2},{1,3},{2,0},{3,1},{4,6},{5,7},{6,4},{7,5},{8,10},{9,11},{10,... | collective-permute-start | bytes 786440 | tf_op jit(solution)/shard_map/ppermute | solution.py:253
  58.1 4.7 %collective-permute-done.22 = bf16[256,512]{1,0:T(8,128)(2,1)S(1)} collective-permute-done((bf16[256,512]{1,0:T(8,128)(2,1)S(1)}, bf16[256,512]{1,0:T(8,128)(2,1)S(1)}, u32[]{:S(2)}, u32[]{:S(2)}) %collective-permute-start.22) | collective-permute-done | bytes 262176 | tf_op jit(solution)/shard_map/ppermute | solution.py:253
  63.8 2.1 collective-permute-done.27
  72.4 12.8 %collective-permute-done.11 = bf16[512,512]{1,0:T(8,128)(2,1)S(1)} collective-permute-done((bf16[512,512]{1,0:T(8,128)(2,1)S(1)}, bf16[512,512]{1,0:T(8,128)(2,1)S(1)}, u32[]{:S(2)}, u32[]{:S(2)}) %collective-permute-start.11) | collective-permute-done | bytes 524320 | tf_op jit(solution)/shard_map/ppermute | solution.py:291
  87.4 4.6 %collective-permute-done.19 = bf16[512,512]{1,0:T(8,128)(2,1)S(1)} collective-permute-done((bf16[512,512]{1,0:T(8,128)(2,1)S(1)}, bf16[512,512]{1,0:T(8,128)(2,1)S(1)}, u32[]{:S(2)}, u32[]{:S(2)}) %collective-permute-start.19) | collective-permute-done | bytes 524320 | tf_op jit(solution)/shard_map/ppermute | solution.py:291
  92.5 18.8 %collective-permute-done.24 = bf16[512,512]{1,0:T(8,128)(2,1)S(1)} collective-permute-done((bf16[512,512]{1,0:T(8,128)(2,1)S(1)}, bf16[512,512]{1,0:T(8,128)(2,1)S(1)}, u32[]{:S(2)}, u32[]{:S(2)}) %collective-permute-start.24) | collective-permute-done | bytes 524320 | tf_op jit(solution)/shard_map/ppermute | solution.py:291
  113.4 3.9 %collective-permute-done.29 = bf16[512,512]{1,0:T(8,128)(2,1)S(1)} collective-permute-done((bf16[512,512]{1,0:T(8,128)(2,1)S(1)}, bf16[512,512]{1,0:T(8,128)(2,1)S(1)}, u32[]{:S(2)}, u32[]{:S(2)}) %collective-permute-start.29) | collective-permute-done | bytes 524320 | tf_op jit(solution)/shard_map/ppermute | solution.py:291
  119.6 4.7 %convolution_bitcast_fusion.7.base_ref = f32[1376,512]{1,0:T(8,128)S(1)} fusion(bf16[3,1376,1024]{2,1,0:T(8,128)(2,1)S(1)} %bitcast.93, bf16[3,512]{1,0:T(4,128)(2,1)S(1)} %get-tuple-element.40, bf16[512,1024]{1,0:T(8,128)(2,1)S(1)} %get-tuple-element.24), kind=kOutput, calls=%fused_computation.15 | convolution fusion | flops 4330094592 | bytes 12323840 | tf_op jit(solution)/shard_map/dot_general | solution.py:43
  124.3 4.7 %convolution_bitcast_fusion.3.base_ref = f32[1376,512]{1,0:T(8,128)S(1)} fusion(bf16[3,1376,1024]{2,1,0:T(8,128)(2,1)S(1)} %bitcast.93, bf16[3,512]{1,0:T(4,128)(2,1)S(1)} %get-tuple-element.39, bf16[512,1024]{1,0:T(8,128)(2,1)S(1)} %get-tuple-element.23), kind=kOutput, calls=%fused_computation.11 | convolution fusion | flops 4330094592 | bytes 12323840 | tf_op jit(solution)/shard_map/dot_general | solution.py:43
  130.8 4.8 %fusion.11 = bf16[512,1376]{0,1:T(8,128)(2,1)S(1)} fusion(bf16[3,1376,1024]{2,1,0:T(8,128)(2,1)S(1)} %bitcast.93, bf16[3,512]{1,0:T(4,128)(2,1)S(1)} %get-tuple-element.36, bf16[512,1024]{1,0:T(8,128)(2,1)S(1)} %get-tuple-element.20), kind=kOutput, calls=%fused_computation.25 | convolution fusion | flops 4330799104 | bytes 10914816 | tf_op jit(solution)/shard_map/dot_general | solution.py:43
  139.7 6.0 %fusion.17 = bf16[512,1376]{0,1:T(8,128)(2,1)} fusion(bf16[3,1376,1024]{2,1,0:T(8,128)(2,1)S(1)} %bitcast.93, bf16[3,512]{1,0:T(4,128)(2,1)S(1)} %get-tuple-element.35, bf16[512,1024]{1,0:T(8,128)(2,1)S(1)} %get-tuple-element.19), kind=kOutput, calls=%fused_computation.27 | convolution fusion | flops 4330799104 | bytes 10914816 | tf_op jit(solution)/shard_map/dot_general | solution.py:43
  147.2 4.8 %fusion.8 = bf16[512,1376]{0,1:T(8,128)(2,1)S(1)} fusion(bf16[3,1376,1024]{2,1,0:T(8,128)(2,1)S(1)} %bitcast.93, bf16[3,512]{1,0:T(4,128)(2,1)S(1)} %get-tuple-element.34, bf16[512,1024]{1,0:T(8,128)(2,1)S(1)} %get-tuple-element.18), kind=kOutput, calls=%fused_computation.24 | convolution fusion | flops 4330799104 | bytes 10914816 | tf_op jit(solution)/shard_map/dot_general | solution.py:43
  152.0 4.8 %fusion.14 = bf16[512,1376]{0,1:T(8,128)(2,1)S(1)} fusion(bf16[3,1376,1024]{2,1,0:T(8,128)(2,1)S(1)} %bitcast.93, bf16[3,512]{1,0:T(4,128)(2,1)S(1)} %get-tuple-element.37, bf16[512,1024]{1,0:T(8,128)(2,1)S(1)} %get-tuple-element.21), kind=kOutput, calls=%fused_computation.26 | convolution fusion | flops 4330799104 | bytes 10914816 | tf_op jit(solution)/shard_map/dot_general | solution.py:43
  157.9 11.6 %collective-permute-done.32 = bf16[512,1376]{0,1:T(8,128)(2,1)} collective-permute-done((bf16[512,1376]{0,1:T(8,128)(2,1)S(1)}, bf16[512,1376]{0,1:T(8,128)(2,1)}, u32[]{:S(2)}, u32[]{:S(2)}) %collective-permute-start.32) | collective-permute-done | bytes 1409056 | tf_op jit(solution)/shard_map/ppermute | solution.py:250
  171.1 6.1 %add_convert_fusion.1 = bf16[512,1376]{0,1:T(8,128)(2,1)S(1)} fusion(bf16[512,1376]{0,1:T(8,128)(2,1)} %collective-permute-done.32, bf16[3,1376,1024]{2,1,0:T(8,128)(2,1)S(1)} %bitcast.93, bf16[3,512]{1,0:T(4,128)(2,1)S(1)} %get-tuple-element.38, bf16[512,1024]{1,0:T(8,128)(2,1)S(1)} %get-tuple-element.22), kind=kOutput, calls=%fused_computation.39 | convolution fusion | flops 4332208128 | bytes 12323840 | tf_op jit(solution)/shard_map/dot_general | solution.py:43
  177.1 2.7 collective-permute-done.35
  180.3 6.9 %add_convert_fusion = bf16[512,1376]{0,1:T(8,128)(2,1)} fusion(bf16[512,1376]{0,1:T(8,128)(2,1)} %collective-permute-done.35, bf16[3,1376,1024]{2,1,0:T(8,128)(2,1)S(1)} %bitcast.93, bf16[3,512]{1,0:T(4,128)(2,1)S(1)} %get-tuple-element.33, bf16[512,1024]{1,0:T(8,128)(2,1)S(1)} %get-tuple-element.17), kind=kOutput, calls=%fused_computation.38 | convolution fusion | flops 4332208128 | bytes 12323840 | tf_op jit(solution)/shard_map/dot_general | solution.py:43
  188.8 10.8 %collective-permute-done.3.refs_5_ = bf16[1376,512]{1,0:T(8,128)(2,1)S(1)} collective-permute-done((bf16[1376,512]{1,0:T(8,128)(2,1)S(1)}, bf16[1376,512]{1,0:T(8,128)(2,1)S(1)}, u32[]{:S(2)}, u32[]{:S(2)}) %collective-permute-start.3) | collective-permute-done | bytes 1409056 | tf_op jit(solution)/shard_map/ppermute | solution.py:250
  202.2 7.8 %collective-permute-done.4.refs_6_ = bf16[1376,512]{1,0:T(8,128)(2,1)} collective-permute-done((bf16[1376,512]{1,0:T(8,128)(2,1)}, bf16[1376,512]{1,0:T(8,128)(2,1)}, u32[]{:S(2)}, u32[]{:S(2)}) %collective-permute-start.4) | collective-permute-done | bytes 1409056 | tf_op jit(solution)/shard_map/ppermute | solution.py:250
  210.5 19.4 %collective-permute-done.5.refs_7_ = bf16[1376,512]{1,0:T(8,128)(2,1)} collective-permute-done((bf16[1376,512]{1,0:T(8,128)(2,1)}, bf16[1376,512]{1,0:T(8,128)(2,1)}, u32[]{:S(2)}, u32[]{:S(2)}) %collective-permute-start.5) | collective-permute-done | bytes 1409056 | tf_op jit(solution)/shard_map/ppermute | solution.py:250
  231.3 46.2 %shard_map.85 = f32[3,1376,1024]{2,1,0:T(8,128)} custom-call(bf16[1376,512]{1,0:T(8,128)(2,1)S(1)} %get-tuple-element.16.refs_0_, bf16[1376,512]{1,0:T(8,128)(2,1)S(1)} %get-tuple-element.15.refs_1_, bf16[1376,512]{1,0:T(8,128)(2,1)} %collective-permute-done.refs_2_, bf16[1376,512]{1,0:T(8,128)(2,1)} %collective-permute-done.1.refs_3_, ...), custom_call_target="tpu_custom_call" | custom-call | flops 34628173824 | bytes 36569088 | tf_op jit(solution)/shard_map/pallas_call | solution.py:163
  277.5 12.2 %collective-permute-done.36 = bf16[512,1376]{0,1:T(8,128)(2,1)S(1)} collective-permute-done((bf16[512,1376]{0,1:T(8,128)(2,1)}, bf16[512,1376]{0,1:T(8,128)(2,1)S(1)}, u32[]{:S(2)}, u32[]{:S(2)}) %collective-permute-start.36) | collective-permute-done | bytes 1409056 | tf_op jit(solution)/shard_map/ppermute | solution.py:250
  289.7 3.6 %shard_map.87 = (bf16[1376,1024]{1,0:T(8,128)(2,1)}, bf16[1376,1024]{1,0:T(8,128)(2,1)}) custom-call(f32[1376,512]{1,0:T(8,128)S(1)} %convolution_bitcast_fusion.3.base_ref, bf16[1376,512]{1,0:T(8,128)(2,1)S(1)} %bitcast.95, bf16[1376,512]{1,0:T(8,128)(2,1)S(1)} %bitcast.96, bf16[1376,1024]{1,0:T(8,128)(2,1)S(1)} %bitcast.90, bf16[1376,1024]{1,0:T(8,128)(2,1)S(1)} %bitcast.87), custom_call_target="tpu_custom_call" | custom-call | flops 14090240 | bytes 11272192 | tf_op jit(solution)/shard_map/pallas_call | solution.py:216
  293.3 4.8 %shard_map.88 = (bf16[1376,1024]{1,0:T(8,128)(2,1)}, bf16[1376,1024]{1,0:T(8,128)(2,1)}) custom-call(f32[1376,512]{1,0:T(8,128)S(1)} %convolution_bitcast_fusion.7.base_ref, bf16[1376,512]{1,0:T(8,128)(2,1)} %bitcast.22.direct_ref, bf16[1376,512]{1,0:T(8,128)(2,1)S(1)} %bitcast.94, ...), custom_call_target="tpu_custom_call", output_to_operand_aliasing={{0}: (5, {}), {1}: (6, {})} | custom-call | flops 14090240 | bytes 11272192 | tf_op jit(solution)/shard_map/pallas_call | solution.py:216
  (115 shorter events, 45.8 us)
Async XLA Ops:
  0.6 23.6 %collective-permute-start.15 = (s32[1024]{0:T(1024)}, s32[1024]{0:T(1024)S(1)}, u32[]{:S(2)}, u32[]{:S(2)}) collective-permute-start(s32[1024]{0:T(1024)} %param.6), channel_id=1, source_target_pairs={{0,24},{8,16},{16,8},{24,0},{1,25},{9,17},{17,9},{25,1},{2,26},{10... | collective-permute-start | bytes 12296 | tf_op jit(solution)/shard_map/ppermute | solution.py:250
  4.6 19.5 %collective-permute-start.14 = (s32[1024]{0:T(1024)}, s32[1024]{0:T(1024)S(1)}, u32[]{:S(2)}, u32[]{:S(2)}) collective-permute-start(s32[1024]{0:T(1024)} %param.6), channel_id=1, source_target_pairs={{0,16},{8,24},{16,0},{24,8},{1,17},{9,25},{17,1},{25,9},{2,18},{10... | collective-permute-start | bytes 12296 | tf_op jit(solution)/shard_map/ppermute | solution.py:250
  5.1 19.9 %collective-permute-start.13 = (s32[1024]{0:T(1024)}, s32[1024]{0:T(1024)S(1)}, u32[]{:S(2)}, u32[]{:S(2)}) collective-permute-start(s32[1024]{0:T(1024)} %param.6), channel_id=1, source_target_pairs={{0,8},{8,0},{16,24},{24,16},{1,9},{9,1},{17,25},{25,17},{2,10},{10... | collective-permute-start | bytes 12296 | tf_op jit(solution)/shard_map/ppermute | solution.py:250
  8.8 178.4 %collective-permute-start = (bf16[1376,512]{1,0:T(8,128)(2,1)S(1)}, bf16[1376,512]{1,0:T(8,128)(2,1)}, u32[]{:S(2)}, u32[]{:S(2)}) collective-permute-start(bf16[1376,512]{1,0:T(8,128)(2,1)S(1)} %get-tuple-element.16.refs_0_), channel_id=1, source_target_pairs={{0,8},{8,0},{16,24},{24,16},{1,9},{9,1},{17,25},{25,17},{2,10},{10... | collective-permute-start | bytes 4227080 | tf_op jit(solution)/shard_map/ppermute | solution.py:250
  12.8 12.3 %collective-permute-start.8 = (bf16[256,512]{1,0:T(8,128)(2,1)}, bf16[256,512]{1,0:T(8,128)(2,1)}, u32[]{:S(2)}, u32[]{:S(2)}) collective-permute-start(bf16[256,512]{1,0:T(8,128)(2,1)} %get-tuple-element.30), channel_id=1, source_target_pairs={{0,6},{1,7},{2,4},{3,5},{4,2},{5,3},{6,0},{7,1},{8,14},{9,15},{10,... | collective-permute-start | bytes 786440 | tf_op jit(solution)/shard_map/ppermute | solution.py:253
  24.2 13.7 %collective-permute-start.7 = (bf16[256,512]{1,0:T(8,128)(2,1)}, bf16[256,512]{1,0:T(8,128)(2,1)S(1)}, u32[]{:S(2)}, u32[]{:S(2)}) collective-permute-start(bf16[256,512]{1,0:T(8,128)(2,1)} %get-tuple-element.31), channel_id=1, source_target_pairs={{0,4},{1,5},{2,6},{3,7},{4,0},{5,1},{6,2},{7,3},{8,12},{9,13},{10,... | collective-permute-start | bytes 786440 | tf_op jit(solution)/shard_map/ppermute | solution.py:253
  24.2 13.6 %collective-permute-start.6 = (bf16[256,512]{1,0:T(8,128)(2,1)S(1)}, bf16[256,512]{1,0:T(8,128)(2,1)S(1)}, u32[]{:S(2)}, u32[]{:S(2)}) collective-permute-start(bf16[256,512]{1,0:T(8,128)(2,1)S(1)} %get-tuple-element.32), channel_id=1, source_target_pairs={{0,2},{1,3},{2,0},{3,1},{4,6},{5,7},{6,4},{7,5},{8,10},{9,11},{10,... | collective-permute-start | bytes 786440 | tf_op jit(solution)/shard_map/ppermute | solution.py:253
  39.6 10.7 %collective-permute-start.9 = (bf16[256,512]{1,0:T(8,128)(2,1)S(1)}, bf16[256,512]{1,0:T(8,128)(2,1)S(1)}, u32[]{:S(2)}, u32[]{:S(2)}) collective-permute-start(bf16[256,512]{1,0:T(8,128)(2,1)S(1)} %get-tuple-element.28), channel_id=1, source_target_pairs={{0,2},{1,3},{2,0},{3,1},{4,6},{5,7},{6,4},{7,5},{8,10},{9,11},{10,... | collective-permute-start | bytes 786440 | tf_op jit(solution)/shard_map/ppermute | solution.py:253
  39.6 11.9 %collective-permute-start.21 = (bf16[256,512]{1,0:T(8,128)(2,1)S(1)}, bf16[256,512]{1,0:T(8,128)(2,1)S(1)}, u32[]{:S(2)}, u32[]{:S(2)}) collective-permute-start(bf16[256,512]{1,0:T(8,128)(2,1)S(1)} %get-tuple-element.26), channel_id=1, source_target_pairs={{0,16},{8,24},{16,0},{24,8},{1,17},{9,25},{17,1},{25,9},{2,18},{10... | collective-permute-start | bytes 786440 | tf_op jit(solution)/shard_map/ppermute | solution.py:250
  41.2 14.6 %collective-permute-start.26 = (bf16[256,512]{1,0:T(8,128)(2,1)S(1)}, bf16[256,512]{1,0:T(8,128)(2,1)S(1)}, u32[]{:S(2)}, u32[]{:S(2)}) collective-permute-start(bf16[256,512]{1,0:T(8,128)(2,1)S(1)} %get-tuple-element.25), channel_id=1, source_target_pairs={{0,24},{8,16},{16,8},{24,0},{1,25},{9,17},{17,9},{25,1},{2,26},{10... | collective-permute-start | bytes 786440 | tf_op jit(solution)/shard_map/ppermute | solution.py:250
  50.6 16.2 %collective-permute-start.10 = (bf16[512,512]{1,0:T(8,128)(2,1)S(1)}, bf16[512,512]{1,0:T(8,128)(2,1)S(1)}, u32[]{:S(2)}, u32[]{:S(2)}) collective-permute-start(bf16[512,512]{1,0:T(8,128)(2,1)S(1)} %maximum_select_fusion.8), channel_id=1, source_target_pairs={{2,4},{3,5},{4,2},{5,3},{10,12},{11,13},{12,10},{13,11},{18,20},{1... | collective-permute-start | bytes 1572872 | tf_op jit(solution)/shard_map/ppermute | solution.py:290
  51.5 11.4 %collective-permute-start.22 = (bf16[256,512]{1,0:T(8,128)(2,1)S(1)}, bf16[256,512]{1,0:T(8,128)(2,1)S(1)}, u32[]{:S(2)}, u32[]{:S(2)}) collective-permute-start(bf16[256,512]{1,0:T(8,128)(2,1)S(1)} %collective-permute-done.21), channel_id=1, source_target_pairs={{0,2},{1,3},{2,0},{3,1},{4,6},{5,7},{6,4},{7,5},{8,10},{9,11},{10,... | collective-permute-start | bytes 786440 | tf_op jit(solution)/shard_map/ppermute | solution.py:253
  55.8 10.0 %collective-permute-start.27 = (bf16[256,512]{1,0:T(8,128)(2,1)S(1)}, bf16[256,512]{1,0:T(8,128)(2,1)S(1)}, u32[]{:S(2)}, u32[]{:S(2)}) collective-permute-start(bf16[256,512]{1,0:T(8,128)(2,1)S(1)} %collective-permute-done.26), channel_id=1, source_target_pairs={{0,2},{1,3},{2,0},{3,1},{4,6},{5,7},{6,4},{7,5},{8,10},{9,11},{10,... | collective-permute-start | bytes 786440 | tf_op jit(solution)/shard_map/ppermute | solution.py:253
  57.3 10.8 %collective-permute-start.18 = (bf16[512,512]{1,0:T(8,128)(2,1)S(1)}, bf16[512,512]{1,0:T(8,128)(2,1)S(1)}, u32[]{:S(2)}, u32[]{:S(2)}) collective-permute-start(bf16[512,512]{1,0:T(8,128)(2,1)S(1)} %maximum_select_fusion.9), channel_id=1, source_target_pairs={{2,4},{3,5},{4,2},{5,3},{10,12},{11,13},{12,10},{13,11},{18,20},{1... | collective-permute-start | bytes 1572872 | tf_op jit(solution)/shard_map/ppermute | solution.py:290
  66.8 18.5 %collective-permute-start.11 = (bf16[512,512]{1,0:T(8,128)(2,1)S(1)}, bf16[512,512]{1,0:T(8,128)(2,1)S(1)}, u32[]{:S(2)}, u32[]{:S(2)}) collective-permute-start(bf16[512,512]{1,0:T(8,128)(2,1)S(1)} %collective-permute-done.10), channel_id=1, source_target_pairs={{2,0},{3,1},{4,6},{5,7},{10,8},{11,9},{12,14},{13,15},{18,16},{19,... | collective-permute-start | bytes 1572872 | tf_op jit(solution)/shard_map/ppermute | solution.py:291
  68.1 23.9 %collective-permute-start.19 = (bf16[512,512]{1,0:T(8,128)(2,1)S(1)}, bf16[512,512]{1,0:T(8,128)(2,1)S(1)}, u32[]{:S(2)}, u32[]{:S(2)}) collective-permute-start(bf16[512,512]{1,0:T(8,128)(2,1)S(1)} %collective-permute-done.18), channel_id=1, source_target_pairs={{2,0},{3,1},{4,6},{5,7},{10,8},{11,9},{12,14},{13,15},{18,16},{19,... | collective-permute-start | bytes 1572872 | tf_op jit(solution)/shard_map/ppermute | solution.py:291
  69.6 87.8 %collective-permute-start.2 = (bf16[1376,512]{1,0:T(8,128)(2,1)S(1)}, bf16[1376,512]{1,0:T(8,128)(2,1)}, u32[]{:S(2)}, u32[]{:S(2)}) collective-permute-start(bf16[1376,512]{1,0:T(8,128)(2,1)S(1)} %get-tuple-element.16.refs_0_), channel_id=1, source_target_pairs={{0,16},{8,24},{16,0},{24,8},{1,17},{9,25},{17,1},{25,9},{2,18},{10... | collective-permute-start | bytes 4227080 | tf_op jit(solution)/shard_map/ppermute | solution.py:250
  71.2 40.2 %collective-permute-start.24 = (bf16[512,512]{1,0:T(8,128)(2,1)S(1)}, bf16[512,512]{1,0:T(8,128)(2,1)S(1)}, u32[]{:S(2)}, u32[]{:S(2)}) collective-permute-start(bf16[512,512]{1,0:T(8,128)(2,1)S(1)} %collective-permute-done.23), channel_id=1, source_target_pairs={{2,0},{3,1},{4,6},{5,7},{10,8},{11,9},{12,14},{13,15},{18,16},{19,... | collective-permute-start | bytes 1572872 | tf_op jit(solution)/shard_map/ppermute | solution.py:291
  85.3 31.9 %collective-permute-start.29 = (bf16[512,512]{1,0:T(8,128)(2,1)S(1)}, bf16[512,512]{1,0:T(8,128)(2,1)S(1)}, u32[]{:S(2)}, u32[]{:S(2)}) collective-permute-start(bf16[512,512]{1,0:T(8,128)(2,1)S(1)} %collective-permute-done.28), channel_id=1, source_target_pairs={{2,0},{3,1},{4,6},{5,7},{10,8},{11,9},{12,14},{13,15},{18,16},{19,... | collective-permute-start | bytes 1572872 | tf_op jit(solution)/shard_map/ppermute | solution.py:291
  92.0 25.7 %collective-permute-start.12 = (bf16[1024,512]{1,0:T(8,128)(2,1)S(1)}, bf16[1024,512]{1,0:T(8,128)(2,1)S(1)}, u32[]{:S(2)}, u32[]{:S(2)}) collective-permute-start(bf16[1024,512]{1,0:T(8,128)(2,1)S(1)} %maximum_select_fusion.4), channel_id=1, source_target_pairs={{0,1},{1,0},{2,3},{3,2},{4,5},{5,4},{6,7},{7,6},{8,9},{9,8},{10,11... | collective-permute-start | bytes 3145736 | tf_op jit(solution)/shard_map/ppermute | solution.py:253
  111.3 45.4 %collective-permute-start.1 = (bf16[1376,512]{1,0:T(8,128)(2,1)S(1)}, bf16[1376,512]{1,0:T(8,128)(2,1)}, u32[]{:S(2)}, u32[]{:S(2)}) collective-permute-start(bf16[1376,512]{1,0:T(8,128)(2,1)S(1)} %get-tuple-element.15.refs_1_), channel_id=1, source_target_pairs={{0,8},{8,0},{16,24},{24,16},{1,9},{9,1},{17,25},{25,17},{2,10},{10... | collective-permute-start | bytes 4227080 | tf_op jit(solution)/shard_map/ppermute | solution.py:250
  117.2 21.2 %collective-permute-start.20 = (bf16[1024,512]{1,0:T(8,128)(2,1)S(1)}, bf16[1024,512]{1,0:T(8,128)(2,1)S(1)}, u32[]{:S(2)}, u32[]{:S(2)}) collective-permute-start(bf16[1024,512]{1,0:T(8,128)(2,1)S(1)} %maximum_select_fusion.5), channel_id=1, source_target_pairs={{0,1},{1,0},{2,3},{3,2},{4,5},{5,4},{6,7},{7,6},{8,9},{9,8},{10,11... | collective-permute-start | bytes 3145736 | tf_op jit(solution)/shard_map/ppermute | solution.py:253
  117.8 11.2 %collective-permute-start.30 = (bf16[1024,512]{1,0:T(8,128)(2,1)S(1)}, bf16[1024,512]{1,0:T(8,128)(2,1)S(1)}, u32[]{:S(2)}, u32[]{:S(2)}) collective-permute-start(bf16[1024,512]{1,0:T(8,128)(2,1)S(1)} %maximum_select_fusion.7), channel_id=1, source_target_pairs={{0,1},{1,0},{2,3},{3,2},{4,5},{5,4},{6,7},{7,6},{8,9},{9,8},{10,11... | collective-permute-start | bytes 3145736 | tf_op jit(solution)/shard_map/ppermute | solution.py:253
  135.6 33.9 %collective-permute-start.32 = (bf16[512,1376]{0,1:T(8,128)(2,1)S(1)}, bf16[512,1376]{0,1:T(8,128)(2,1)}, u32[]{:S(2)}, u32[]{:S(2)}) collective-permute-start(bf16[512,1376]{0,1:T(8,128)(2,1)S(1)} %fusion.11), channel_id=1, source_target_pairs={{0,16},{8,24},{16,0},{24,8},{1,17},{9,25},{17,1},{25,9},{2,18},{10... | collective-permute-start | bytes 4227080 | tf_op jit(solution)/shard_map/ppermute | solution.py:250
  145.7 34.1 %collective-permute-start.35 = (bf16[512,1376]{0,1:T(8,128)(2,1)}, bf16[512,1376]{0,1:T(8,128)(2,1)}, u32[]{:S(2)}, u32[]{:S(2)}) collective-permute-start(bf16[512,1376]{0,1:T(8,128)(2,1)} %fusion.17), channel_id=1, source_target_pairs={{0,8},{8,0},{16,24},{24,16},{1,9},{9,1},{17,25},{25,17},{2,10},{10... | collective-permute-start | bytes 4227080 | tf_op jit(solution)/shard_map/ppermute | solution.py:250
  156.8 42.9 %collective-permute-start.3 = (bf16[1376,512]{1,0:T(8,128)(2,1)S(1)}, bf16[1376,512]{1,0:T(8,128)(2,1)S(1)}, u32[]{:S(2)}, u32[]{:S(2)}) collective-permute-start(bf16[1376,512]{1,0:T(8,128)(2,1)S(1)} %get-tuple-element.15.refs_1_), channel_id=1, source_target_pairs={{0,16},{8,24},{16,0},{24,8},{1,17},{9,25},{17,1},{25,9},{2,18},{10... | collective-permute-start | bytes 4227080 | tf_op jit(solution)/shard_map/ppermute | solution.py:250
  157.4 52.6 %collective-permute-start.4 = (bf16[1376,512]{1,0:T(8,128)(2,1)}, bf16[1376,512]{1,0:T(8,128)(2,1)}, u32[]{:S(2)}, u32[]{:S(2)}) collective-permute-start(bf16[1376,512]{1,0:T(8,128)(2,1)} %collective-permute-done.2.refs_4_), channel_id=1, source_target_pairs={{0,8},{8,0},{16,24},{24,16},{1,9},{9,1},{17,25},{25,17},{2,10},{10... | collective-permute-start | bytes 4227080 | tf_op jit(solution)/shard_map/ppermute | solution.py:250
  169.6 60.4 %collective-permute-start.5 = (bf16[1376,512]{1,0:T(8,128)(2,1)}, bf16[1376,512]{1,0:T(8,128)(2,1)}, u32[]{:S(2)}, u32[]{:S(2)}) collective-permute-start(bf16[1376,512]{1,0:T(8,128)(2,1)} %collective-permute-done.1.refs_3_), channel_id=1, source_target_pairs={{0,16},{8,24},{16,0},{24,8},{1,17},{9,25},{17,1},{25,9},{2,18},{10... | collective-permute-start | bytes 4227080 | tf_op jit(solution)/shard_map/ppermute | solution.py:250
  179.8 113.5 %collective-permute-start.31 = (bf16[512,1376]{0,1:T(8,128)(2,1)S(1)}, bf16[512,1376]{0,1:T(8,128)(2,1)}, u32[]{:S(2)}, u32[]{:S(2)}) collective-permute-start(bf16[512,1376]{0,1:T(8,128)(2,1)S(1)} %fusion.8), channel_id=1, source_target_pairs={{0,16},{8,24},{16,0},{24,8},{1,17},{9,25},{17,1},{25,9},{2,18},{10... | collective-permute-start | bytes 4227080 | tf_op jit(solution)/shard_map/ppermute | solution.py:250
  187.3 90.3 %collective-permute-start.34 = (bf16[512,1376]{0,1:T(8,128)(2,1)S(1)}, bf16[512,1376]{0,1:T(8,128)(2,1)S(1)}, u32[]{:S(2)}, u32[]{:S(2)}) collective-permute-start(bf16[512,1376]{0,1:T(8,128)(2,1)S(1)} %fusion.14), channel_id=1, source_target_pairs={{0,8},{8,0},{16,24},{24,16},{1,9},{9,1},{17,25},{25,17},{2,10},{10... | collective-permute-start | bytes 4227080 | tf_op jit(solution)/shard_map/ppermute | solution.py:250
  200.7 92.6 %collective-permute-start.33 = (bf16[512,1376]{0,1:T(8,128)(2,1)S(1)}, bf16[512,1376]{0,1:T(8,128)(2,1)S(1)}, u32[]{:S(2)}, u32[]{:S(2)}) collective-permute-start(bf16[512,1376]{0,1:T(8,128)(2,1)S(1)} %add_convert_fusion.1), channel_id=1, source_target_pairs={{0,8},{8,0},{16,24},{24,16},{1,9},{9,1},{17,25},{25,17},{2,10},{10... | collective-permute-start | bytes 4227080 | tf_op jit(solution)/shard_map/ppermute | solution.py:250
  210.0 79.7 %collective-permute-start.36 = (bf16[512,1376]{0,1:T(8,128)(2,1)}, bf16[512,1376]{0,1:T(8,128)(2,1)S(1)}, u32[]{:S(2)}, u32[]{:S(2)}) collective-permute-start(bf16[512,1376]{0,1:T(8,128)(2,1)} %add_convert_fusion), channel_id=1, source_target_pairs={{0,16},{8,24},{16,0},{24,8},{1,17},{9,25},{17,1},{25,9},{2,18},{10... | collective-permute-start | bytes 4227080 | tf_op jit(solution)/shard_map/ppermute | solution.py:250
  (15 other events, 303.8 us)
